TPU v7x, 32 devices: a whole 2x2x4 slice. The times are simulated.
32 devices in a mesh: graphs: 2 (over y), rows: 4 (over z), cols: 2 (over x), sub: 2 (over core).
Axes of the slice: x: 2, y: 2, z: 4, core: 2. Of those that a mesh axis runs over, the one named last changes fastest.
Arguments:
- current_block: float32 [16, 65536], P(None, ('graphs', 'rows', 'cols', 'sub')), parts along dimension 1, may hold values from -1200 to 1200, as said below
- previous_block: float32 [16, 65536], P(None, ('graphs', 'rows', 'cols', 'sub')), parts along dimension 1, may hold values from -1200 to 1200, as said below
- adjacency_tiles: float32 [1536, 128, 128], P(('graphs', 'rows', 'cols', 'sub')), parts along dimension 0, may hold values from -0.3125 to 0.3125
- tile_rows: int32 [1536], P(('graphs', 'rows', 'cols', 'sub')), parts along dimension 0, may hold values from 0 to 255, as said below
- tile_cols: int32 [1536], P(('graphs', 'rows', 'cols', 'sub')), parts along dimension 0, may hold values from 0 to 255, as said below
- tile_count: int32 [32], P(('graphs', 'rows', 'cols', 'sub')), parts along dimension 0, may hold values from 18 to 48, as said below
- locked: int32 [2], P('graphs'), parts along dimension 0, may hold values from 0 to 7
Outputs:
- w_basis: float32 [16, 65536], P(None, ('graphs', 'rows', 'cols', 'sub')), parts along dimension 1
- w_image: float32 [16, 65536], P(None, ('graphs', 'rows', 'cols', 'sub')), parts along dimension 1
- ritz_matrix: float32 [96, 48], P('graphs'), parts along dimension 0
There are 2 independent parts, one for each index of `graphs`. A program takes and returns all parts, laid end to end along the dimension named above; each array names one. Nothing has to cross between parts.
Inputs may be any that keep to these rules, and one draw needn't show every extreme that they name: `current_block`: entries of order one to some hundreds. `previous_block`: entries of order one to some hundreds. Slots d * 48 to (d + 1) * 48 - 1 belong to device d and name its own tile rows d * 16 to (d + 1) * 16 - 1. The first 16 slots of a device name its tile rows in order, with tile_cols equal to tile_rows. Slots past the device's count name tile row d * 16 and carry no weight. `tile_cols`: A slot of device d names a tile column from d * 16 - 8 to (d + 1) * 16 + 7. Slot 16 of a device names a tile of the block before it and slot 17 one of the block after it, where such a block exists. A pair of tile row and tile column may stand in several slots; their tiles add. `tile_count`: in every draw some device has all 48 slots live.
All inputs are finite; a program needn't handle non-finite values.
Results may differ from a plain program's by a relative error of at most 0.000094.
Values sent between devices are 32-bit elements; how exact they have to be, the bound alone decides.
No kernel may reach another device: no remote copies, remote signals or barrier semaphores. Data moves between devices by JAX's collectives and lax.ppermute only.
A program may use at most 64 MiB of HBM per device.

v0:
```python
import jax
import jax.numpy as jnp
from jax import lax
from jax.sharding import PartitionSpec as P


def extended(cells, sides, width):
    for axis, dim in sides:
        count = lax.axis_size(axis)
        ends = count - 1
        head = lax.slice_in_dim(cells, 0, width, axis=dim)
        tail = lax.slice_in_dim(cells, cells.shape[dim] - width, cells.shape[dim], axis=dim)
        cells = jnp.concatenate(
            [
                lax.ppermute(tail, axis, [(i, (i + 1) % count) for i in range(ends)]),
                cells,
                lax.ppermute(head, axis, [((i + 1) % count, i) for i in range(ends)]),
            ],
            axis=dim,
        )
    return cells


def inner_products(left, right):
    return jnp.dot(left, right.T, precision=lax.Precision.HIGHEST)


def solve_lower(factor, values):
    return lax.linalg.triangular_solve(factor, values, left_side=True, lower=True)


def rayleigh_ritz(gram_b, gram_a):
    factor_b = jnp.linalg.cholesky(gram_b)
    symmetric = 0.5 * (gram_a + gram_a.T)
    halfway = solve_lower(factor_b, symmetric)
    return solve_lower(factor_b, halfway.T)


def operate(vectors, padded, adjacency_tiles, column_position, placing, span_tiles):
    channels, rows_here = vectors.shape
    tile_size = adjacency_tiles.shape[1]
    column_blocks = padded.reshape(channels, span_tiles, tile_size)
    gathered = jnp.take(column_blocks, column_position, axis=1)
    products = jnp.einsum(
        "cta,tab->ctb", gathered, adjacency_tiles, precision=lax.Precision.HIGHEST
    )
    summed = jnp.einsum("ctb,tr->crb", products, placing, precision=lax.Precision.HIGHEST)
    return vectors - summed.reshape(channels, rows_here)


def body(current_block, previous_block, adjacency_tiles, tile_rows, tile_cols, tile_count, locked):
    vectors_k, rows_here = current_block.shape
    tile_size = adjacency_tiles.shape[1]
    row_tiles = rows_here // tile_size
    slot_count = adjacency_tiles.shape[0]
    vertex_total = rows_here * lax.axis_size(("rows", "cols", "sub"))
    position = lax.axis_index(("rows", "cols", "sub"))
    reach_tiles = row_tiles // 2
    span_tiles = row_tiles + 2 * reach_tiles
    column_position = tile_cols - (position * row_tiles - reach_tiles)
    row_slot = tile_rows - position * row_tiles
    live_mask = (jnp.arange(slot_count, dtype=jnp.int32) < tile_count[0]).astype(jnp.float32)
    placing = (row_slot[:, None] == jnp.arange(row_tiles, dtype=jnp.int32)[None, :]).astype(
        jnp.float32
    )
    placing = placing * live_mask[:, None]
    stacked = jnp.concatenate([current_block, previous_block], axis=0)
    padded_pair = extended(stacked, ((("rows", "cols", "sub"), 1),), reach_tiles * tile_size)
    pair_image = operate(
        stacked, padded_pair, adjacency_tiles, column_position, placing, span_tiles
    )
    x_image = pair_image[:vectors_k]
    p_image = pair_image[vectors_k:]
    frozen_rows = jnp.arange(vectors_k, dtype=jnp.int32) < locked[0]
    frozen_diag = jnp.diag(frozen_rows.astype(jnp.float32))
    zero_rows = jnp.zeros((vectors_k,), jnp.float32)
    pad_diag = jnp.diag(jnp.concatenate([zero_rows, frozen_rows.astype(jnp.float32), zero_rows]))
    cross_sum, square_sum = lax.psum(
        (jnp.sum(current_block * x_image, axis=1), jnp.sum(current_block * current_block, axis=1)),
        ("rows", "cols", "sub"),
    )
    quotient = cross_sum / (square_sum + 1e-06)
    residual = jnp.where(frozen_rows[:, None], 0.0, x_image - quotient[:, None] * current_block)
    gram_w = (
        lax.psum(inner_products(residual, residual), ("rows", "cols", "sub")) / vertex_total
        + frozen_diag
    )
    factor = jnp.linalg.cholesky(gram_w)
    w_basis = solve_lower(factor, residual)
    padded = extended(w_basis, ((("rows", "cols", "sub"), 1),), reach_tiles * tile_size)
    w_image = operate(w_basis, padded, adjacency_tiles, column_position, placing, span_tiles)
    search = jnp.concatenate([current_block, w_basis, previous_block], axis=0)
    search_image = jnp.concatenate([x_image, w_image, p_image], axis=0)
    plain_sum, image_sum = lax.psum(
        (inner_products(search, search), inner_products(search, search_image)),
        ("rows", "cols", "sub"),
    )
    gram_b = plain_sum / vertex_total + pad_diag
    gram_a = image_sum / vertex_total
    ritz_matrix = rayleigh_ritz(gram_b, gram_a)
    return (w_basis, w_image, ritz_matrix)


def solution(mesh):
    in_specs = (
        P(None, ("graphs", "rows", "cols", "sub")),
        P(None, ("graphs", "rows", "cols", "sub")),
        P(("graphs", "rows", "cols", "sub"), None, None),
        P(("graphs", "rows", "cols", "sub")),
        P(("graphs", "rows", "cols", "sub")),
        P(("graphs", "rows", "cols", "sub")),
        P("graphs"),
    )
    out_specs = (
        P(None, ("graphs", "rows", "cols", "sub")),
        P(None, ("graphs", "rows", "cols", "sub")),
        P("graphs", None),
    )
    return jax.shard_map(body, mesh=mesh, in_specs=in_specs, out_specs=out_specs, check_vma=False)
```

profile of v0, /device:TPU:0, one launch (start us, length us, event | category | flops | bytes accessed | tf_op | source)
XLA Modules:
  0.0 182.3 jit_solution(9188400379763008146)
XLA Ops:
  0.6 1.1 constant_dynamic-update-slice_fusion.1
  1.7 0.9 constant_dynamic-update-slice_fusion
  3.3 3.0 %collective-permute-start = (f32[32,1024]{1,0:T(8,128)}, f32[32,1024]{1,0:T(8,128)}, u32[]{:S(2)}, u32[]{:S(2)}) collective-permute-start(f32[32,1024]{1,0:T(8,128)} %get-tuple-element.14), channel_id=1, source_target_pairs={{0,1},{1,2},{2,3},{3,4},{4,5},{5,6},{6,7},{7,8},{8,9},{9,10},{10,1... | collective-permute-start | bytes 393224 | tf_op jit(solution)/shard_map/ppermute | solution.py:15
  6.4 1.3 collective-permute-start.1
  11.5 1.8 %copy_bitcast_fusion = f32[32,32,128]{2,0,1:T(8,128)} fusion(f32[32,1024]{1,0:T(8,128)} %collective-permute-done.1, f32[32,2048]{1,0:T(8,128)S(1)} %constant_dynamic-update-slice_fusion, f32[32,1024]{1,0:T(8,128)} %collective-permute-done), kind=kLoop, calls=%fused_computation.9 | loop fusion | flops 262144 | bytes 1048576 | tf_op jit(solution)/shard_map/reshape | solution.py:42
  13.3 2.5 %gather_fusion = f32[48,32,128]{2,1,0:T(8,128)} fusion(f32[32,32,128]{2,0,1:T(8,128)} %copy_bitcast_fusion, s32[1024]{0:T(1024)S(1)} %pad_clamp_fusion), kind=kCustom, calls=%fused_computation | custom fusion | bytes 1573056 | tf_op jit(solution)/shard_map/jit(_take)/gather | solution.py:43
  15.8 4.0 %fusion.2 = f32[48,32,128]{2,1,0:T(8,128)S(1)} fusion(f32[48,128,128]{2,1,0:T(8,128)S(1)} %copy-done, f32[48,32,128]{2,1,0:T(8,128)} %gather_fusion, pred[48]{0:T(512)(128)(4,1)S(1)} %get-tuple-element.10), kind=kOutput, calls=%fused_computation.5 | convolution fusion | flops 302186496 | bytes 4718640 | tf_op jit(solution)/shard_map/cta,tab->ctb/dot_general | solution.py:44
  19.8 0.9 fusion
  21.5 0.8 multiply_reduce_fusion
  22.4 35.7 %all-reduce.1 = (f32[16]{0:T(128)S(1)}, f32[16]{0:T(128)S(1)}) all-reduce(f32[16]{0:T(128)S(1)} %get-tuple-element.5, f32[16]{0:T(128)S(1)} %get-tuple-element.4), channel_id=1, replica_groups=mesh['graphs'=2,'rows'=4,'cols'=2,'sub'=2] {'rows','cols','sub'}, use_global_device_ids=true, to_apply=%region_1.2 | all-reduce | flops 32 | bytes 256 | tf_op jit(solution)/shard_map/psum | solution.py:78
  58.1 1.3 fusion.53
  59.4 30.0 %psum.37 = f32[16,16]{1,0:T(8,128)S(1)} all-reduce(f32[16,16]{1,0:T(8,128)S(1)} %fusion.53), channel_id=1, replica_groups=mesh['graphs'=2,'rows'=4,'cols'=2,'sub'=2] {'rows','cols','sub'}, use_global_device_ids=true, to_apply=%region_4.5 | all-reduce | flops 256 | bytes 2048 | tf_op jit(solution)/shard_map/psum | solution.py:85
  91.0 1.4 cholesky.31
  93.8 1.2 custom-call.12
  95.0 1.3 fusion.32
  96.3 1.8 collective-permute-start.2
  98.1 1.3 collective-permute-start.3
  99.4 2.0 %fusion.20 = f32[48,48]{0,1:T(8,128)} fusion(f32[16,2048]{1,0:T(8,128)} %param.10, f32[16,2048]{1,0:T(8,128)S(1)} %fusion.32, f32[16,2048]{1,0:T(8,128)S(1)} %copy-done.2), kind=kOutput, calls=%fused_computation.26 | convolution fusion | flops 56819712 | bytes 402432 | tf_op jit(solution)/shard_map/dot_general | solution.py:25
  102.2 2.3 %gather_fusion.1 = f32[48,16,128]{2,1,0:T(8,128)} fusion(f32[16,32,128]{2,0,1:T(8,128)} %copy_bitcast_fusion.1, s32[1024]{0:T(1024)S(1)} %pad_clamp_fusion), kind=kCustom, calls=%fused_computation.1 | custom fusion | bytes 786624 | tf_op jit(solution)/shard_map/jit(_take)/gather | solution.py:43
  104.5 3.8 %fusion.14 = f32[48,16,128]{2,1,0:T(8,128)S(1)} fusion(f32[48,128,128]{2,1,0:T(8,128)S(1)} %copy-done, f32[48,16,128]{2,1,0:T(8,128)} %gather_fusion.1, pred[48]{0:T(512)(128)(4,1)S(1)} %get-tuple-element.10), kind=kOutput, calls=%fused_computation.20 | convolution fusion | flops 151093248 | bytes 3932208 | tf_op jit(solution)/shard_map/cta,tab->ctb/dot_general | solution.py:44
  109.4 1.5 fusion.6
  110.9 60.5 %all-reduce = (f32[48,48]{0,1:T(8,128)S(1)}, f32[48,48]{0,1:T(8,128)S(1)}) all-reduce(f32[48,48]{0,1:T(8,128)S(1)} %fusion.6, f32[48,48]{0,1:T(8,128)} %fusion.20), channel_id=1, replica_groups=mesh['graphs'=2,'rows'=4,'cols'=2,'sub'=2] {'rows','cols','sub'}, use_global_device_ids=true, to_apply=%region_10.11 | all-reduce | flops 4608 | bytes 36864 | tf_op jit(solution)/shard_map/psum | solution.py:94
  171.7 4.4 %cholesky.65 = f32[48,48]{1,0:T(8,128)S(1)} custom-call(f32[48,48]{1,0:T(8,128)S(1)} %fusion.29), custom_call_target="Cholesky" | custom-call | tf_op jit(solution)/shard_map/jit(cholesky)/cholesky | solution.py:33
  177.4 3.7 %custom-call.15 = f32[1,48,48]{1,2,0:T(8,128)S(1)} custom-call(f32[1,48,48]{2,1,0:T(8,128)S(1)} %fusion.23), custom_call_target="InvertDiagBlocksLowerTriangular" | custom-call | tf_op jit(solution)/shard_map/triangular_solve/custom-call.3 | solution.py:29
  (50 shorter events, 11.5 us)
Async XLA Ops:
  0.6 15.2 %copy-start = (f32[48,128,128]{2,1,0:T(8,128)S(1)}, f32[48,128,128]{2,1,0:T(8,128)}, u32[]{:S(2)}) copy-start(f32[48,128,128]{2,1,0:T(8,128)} %param.11) | copy-start | bytes 9437188
  3.3 8.1 %collective-permute-start = (f32[32,1024]{1,0:T(8,128)}, f32[32,1024]{1,0:T(8,128)}, u32[]{:S(2)}, u32[]{:S(2)}) collective-permute-start(f32[32,1024]{1,0:T(8,128)} %get-tuple-element.14), channel_id=1, source_target_pairs={{0,1},{1,2},{2,3},{3,4},{4,5},{5,6},{6,7},{7,8},{8,9},{9,10},{10,1... | collective-permute-start | bytes 393224 | tf_op jit(solution)/shard_map/ppermute | solution.py:15
  6.4 5.1 %collective-permute-start.1 = (f32[32,1024]{1,0:T(8,128)S(1)}, f32[32,1024]{1,0:T(8,128)}, u32[]{:S(2)}, u32[]{:S(2)}) collective-permute-start(f32[32,1024]{1,0:T(8,128)S(1)} %get-tuple-element.15), channel_id=1, source_target_pairs={{1,0},{2,1},{3,2},{4,3},{5,4},{6,5},{7,6},{8,7},{9,8},{10,9},{11,1... | collective-permute-start | bytes 393224 | tf_op jit(solution)/shard_map/ppermute | solution.py:17
  10.1 1.3 copy-start.6
  15.8 5.7 %copy-start.2 = (f32[16,2048]{1,0:T(8,128)S(1)}, f32[16,2048]{1,0:T(8,128)}, u32[]{:S(2)}) copy-start(f32[16,2048]{1,0:T(8,128)} %param.9) | copy-start | bytes 393220
  20.8 0.7 copy-start.1
  96.3 12.5 %copy-start.3 = (f32[16,2048]{1,0:T(8,128)}, f32[16,2048]{1,0:T(8,128)S(1)}, u32[]{:S(2)}) copy-start(f32[16,2048]{1,0:T(8,128)S(1)} %fusion.32) | copy-start | bytes 393220
  96.3 5.2 %collective-permute-start.2 = (f32[16,1024]{1,0:T(8,128)S(1)}, f32[16,1024]{1,0:T(8,128)S(1)}, u32[]{:S(2)}, u32[]{:S(2)}) collective-permute-start(f32[16,1024]{1,0:T(8,128)S(1)} %get-tuple-element.16), channel_id=1, source_target_pairs={{0,1},{1,2},{2,3},{3,4},{4,5},{5,6},{6,7},{7,8},{8,9},{9,10},{10,1... | collective-permute-start | bytes 196616 | tf_op jit(solution)/shard_map/ppermute | solution.py:15
  98.1 3.4 %collective-permute-start.3 = (f32[16,1024]{1,0:T(8,128)S(1)}, f32[16,1024]{1,0:T(8,128)S(1)}, u32[]{:S(2)}, u32[]{:S(2)}) collective-permute-start(f32[16,1024]{1,0:T(8,128)S(1)} %get-tuple-element.17), channel_id=1, source_target_pairs={{1,0},{2,1},{3,2},{4,3},{5,4},{6,5},{7,6},{8,7},{9,8},{10,9},{11,1... | collective-permute-start | bytes 196616 | tf_op jit(solution)/shard_map/ppermute | solution.py:17
  104.5 67.0 %copy-start.5 = (f32[48]{0:T(128)S(1)}, f32[48]{0:T(128)}, u32[]{:S(2)}) copy-start(f32[48]{0:T(128)} %pad_maximum_fusion.3) | copy-start | bytes 580
  108.8 0.7 copy-start.4
where the time goes:
time: 183 us; the launch traced here: 182 us
  blocking collectives  126 us (69%)
  other arithmetic  21 us (11%)
  matrix products  16.3 us (9%)
  local copies, waits for them, and re-layouts  9.1 us (5%)
  starting transfers between devices  7.44 us (4%)
  between operations  2.15 us (1%)
    psum x1, blocking collectives, body(): lax.psum((inner_products(search, search), inner_products(search, search_i...  60.5 us
    psum x1, blocking collectives, body(): lax.psum((jnp.sum(current_block * x_image, axis=1), jnp.sum(current_block...  35.7 us
    psum x1, blocking collectives, body(): lax.psum(inner_products(residual, residual), ('rows', 'cols', 'sub'))  30 us
    dot_general x2, matrix products, operate(): jnp.einsum('cta,tab->ctb', gathered, adjacency_tiles, precision=lax.Preci...  7.77 us
    another operation x4, other arithmetic, solve_lower(): lax.linalg.triangular_solve(factor, values, left_side=True, lower=True)  6.2 us
    another operation x3, other arithmetic, rayleigh_ritz(): factor_b = jnp.linalg.cholesky(gram_b)  5.06 us
    ppermute x2, starting transfers between devices, extended(): lax.ppermute(tail, axis, [(i, (i + 1) % count) for i in range(ends)])  4.87 us
    dot_general x3, matrix products, inner_products(): return jnp.dot(left, right.T, precision=lax.Precision.HIGHEST)  4.86 us
  transfers between devices with their start and end apart: 4, of which 0 were waited for; matrix products, arithmetic and copies ran while one was open for 2% of the time, Pallas kernels for 0%

commit v1 on v0

v1 whole, which is shorter than its diff:
```python
import functools

import jax
import jax.numpy as jnp
from jax import lax
from jax.experimental import pallas as pl
from jax.experimental.pallas import tpu as pltpu
from jax.sharding import PartitionSpec as P

AXES = ("rows", "cols", "sub")
F32 = jnp.float32
BF16 = jnp.bfloat16
HIGHEST = lax.Precision.HIGHEST
LANES = 128
UNROLL = 8
VMEM = pl.BlockSpec(memory_space=pltpu.VMEM)
SMEM = pl.BlockSpec(memory_space=pltpu.SMEM)


def split3(x):
    a = x.astype(BF16)
    rest = x - a.astype(F32)
    b = rest.astype(BF16)
    c = (rest - b.astype(F32)).astype(BF16)
    return a, b, c


def store_parts(parts_ref, tile, at, height, values):
    channels = values.shape[0]
    for k, part in enumerate(split3(values)):
        parts_ref[tile, k * height + at : k * height + at + channels, :] = part


def load_span(parts_ref, at, height, left_ref, mid_ref, right_ref, tile):
    reach = left_ref.shape[1] // tile
    rows = mid_ref.shape[1] // tile
    for k in range(reach):
        cut = slice(k * tile, (k + 1) * tile)
        store_parts(parts_ref, k, at, height, left_ref[:, cut])
        store_parts(parts_ref, reach + rows + k, at, height, right_ref[:, cut])
    for k in range(rows):
        store_parts(parts_ref, reach + k, at, height, mid_ref[:, k * tile : (k + 1) * tile])


def tile_product(parts_ref, tiles_ref, t, col, height):
    lhs = parts_ref[col]
    t1, t2, t3 = split3(tiles_ref[t])
    y1 = jnp.dot(lhs, t1, preferred_element_type=F32)
    y2 = jnp.dot(lhs[: 2 * height], t2, preferred_element_type=F32)
    y3 = jnp.dot(lhs[:height], t3, preferred_element_type=F32)
    h = height
    return y1[:h] + ((y1[h : 2 * h] + y2[:h]) + (y1[2 * h :] + y2[h : 2 * h] + y3))


def apply_tiles(parts_ref, sums_ref, tiles_ref, rows_ref, cols_ref, count_ref, height, reach):
    row_tiles = sums_ref.shape[0]
    slots = tiles_ref.shape[0]
    base = rows_ref[0]
    count = count_ref[0]

    def diagonal(step, carry):
        for u in range(UNROLL):
            t = step * UNROLL + u
            sums_ref[t] = tile_product(parts_ref, tiles_ref, t, t + reach, height)
        return carry

    lax.fori_loop(0, row_tiles // UNROLL, diagonal, 0)

    def extra(step, carry):
        found = []
        for u in range(UNROLL):
            t = row_tiles + step * UNROLL + u
            y = tile_product(parts_ref, tiles_ref, t, cols_ref[t] - base + reach, height)
            found.append((rows_ref[t] - base, jnp.where(t < count, y, 0.0)))
        for row, y in found:
            sums_ref[row] += y
        return carry

    lax.fori_loop(0, (slots - row_tiles) // UNROLL, extra, 0)


def first_kernel(tile, rows_ref, cols_ref, count_ref, x_ref, left_ref, right_ref, tiles_ref,
                 image_ref, head_ref, tail_ref, parts_ref, sums_ref):
    channels = x_ref.shape[0]
    reach = left_ref.shape[1] // tile
    row_tiles = sums_ref.shape[0]
    load_span(parts_ref, 0, channels, left_ref, x_ref, right_ref, tile)
    apply_tiles(parts_ref, sums_ref, tiles_ref, rows_ref, cols_ref, count_ref, channels, reach)
    for i in range(row_tiles):
        cut = slice(i * tile, (i + 1) * tile)
        value = x_ref[:, cut] - sums_ref[i]
        image_ref[:, cut] = value
        if i < reach:
            head_ref[:, cut] = value
        if i >= row_tiles - reach:
            k = i - (row_tiles - reach)
            tail_ref[:, k * tile : (k + 1) * tile] = value


def iota2(shape, dim):
    return lax.broadcasted_iota(jnp.int32, shape, dim)


def dot_nt(a, b):
    return lax.dot_general(a, b, (((1,), (1,)), ((), ())), precision=HIGHEST,
                           preferred_element_type=F32)


def second_kernel(tile, rows_ref, cols_ref, count_ref, x_ref, p_ref, pleft_ref, pright_ref,
                  ax_ref, aleft_ref, aright_ref, tiles_ref, a2x_ref, message_ref,
                  parts_ref, sums_ref, basis_ref):
    k = x_ref.shape[0]
    reach = aleft_ref.shape[1] // tile
    row_tiles = sums_ref.shape[0]
    load_span(parts_ref, k, 2 * k, pleft_ref, p_ref, pright_ref, tile)
    load_span(parts_ref, 0, 2 * k, aleft_ref, ax_ref, aright_ref, tile)
    apply_tiles(parts_ref, sums_ref, tiles_ref, rows_ref, cols_ref, count_ref, 2 * k, reach)
    x = x_ref[...]
    ax = ax_ref[...]
    q = jnp.sum(x * ax, axis=1, keepdims=True) / (jnp.sum(x * x, axis=1, keepdims=True) + 1e-06)
    basis_ref[0:k, :] = x
    basis_ref[k : 2 * k, :] = ax - q * x
    basis_ref[2 * k : 3 * k, :] = p_ref[...]
    basis_ref[3 * k : 4 * k, :] = ax
    for i in range(row_tiles):
        cut = slice(i * tile, (i + 1) * tile)
        total = sums_ref[i]
        twice = ax_ref[:, cut] - total[:k]
        a2x_ref[:, cut] = twice
        basis_ref[4 * k : 5 * k, cut] = twice - q * ax_ref[:, cut]
        basis_ref[5 * k : 6 * k, cut] = p_ref[:, cut] - total[k:]
    grams = dot_nt(basis_ref[0 : 3 * k, :], basis_ref[...])
    message_ref[...] = jnp.zeros_like(message_ref)
    message_ref[:, 0 : 6 * k] = grams
    place = iota2((k, LANES), 1) == iota2((k, LANES), 0) + 6 * k
    message_ref[0:k, :] = jnp.where(place, q, message_ref[0:k, :])


def tree(values):
    while len(values) > 1:
        values = [values[i] + values[i + 1] for i in range(0, len(values), 2)]
    return values[0]


def merged(messages, k):
    lane = iota2((k, LANES), 1)
    row = iota2((k, LANES), 0)
    squares, crosses, quotients = [], [], []
    for m in messages:
        top = m[0:k]
        squares.append(jnp.sum(jnp.where(lane == row, top, 0.0), axis=1, keepdims=True))
        crosses.append(jnp.sum(jnp.where(lane == row + 3 * k, top, 0.0), axis=1, keepdims=True))
        quotients.append(jnp.sum(jnp.where(lane == row + 6 * k, top, 0.0), axis=1, keepdims=True))
    q = tree(crosses) / (tree(squares) + 1e-06)
    lane_all = iota2((3 * k, LANES), 1)
    shifted = []
    for m, own in zip(messages, quotients):
        move = own - q
        m = jnp.where(lane_all < 6 * k, m, 0.0)
        m = jnp.concatenate([m[0:k], m[k : 2 * k] + move * m[0:k], m[2 * k :]], axis=0)
        picks = (lane == row) | (lane == row + 3 * k)
        across = jnp.sum(jnp.where(picks, move, 0.0), axis=0, keepdims=True)
        shifted.append(m + pltpu.roll(m * across, k, 1))
    return tree(shifted), q


def merge_kernel(*refs):
    *ins, out_ref = refs
    k = out_ref.shape[0] // 3
    total, q = merged([r[...] for r in ins], k)
    out_ref[...] = total
    place = iota2((k, LANES), 1) == iota2((k, LANES), 0) + 6 * k
    out_ref[0:k, :] = jnp.where(place, q, total[0:k])


def eliminate(matrix):
    n = matrix.shape[0]
    blocks = [matrix[b : b + 8] for b in range(0, n, 8)]
    sub = iota2((8, LANES), 0)
    for j in range(n):
        b0, r0 = divmod(j, 8)
        line = blocks[b0][r0 : r0 + 1]
        pivot = line[:, j : j + 1]
        root = lax.rsqrt(pivot)
        root = root * (1.5 - 0.5 * pivot * root * root)
        line = line * root
        for b in range(b0, len(blocks)):
            update = blocks[b] - (blocks[b][:, j : j + 1] * root) * line
            if b == b0:
                update = jnp.where(sub > r0, update, jnp.where(sub == r0, line, blocks[b]))
            blocks[b] = update
    return jnp.concatenate(blocks, axis=0)


def inverse_factor(gram):
    n = gram.shape[0]
    wide = jnp.concatenate([gram, jnp.zeros((n, LANES - n), F32)], axis=1)
    wide = jnp.where(iota2((n, LANES), 1) == iota2((n, LANES), 0) + n, 1.0, wide)
    done = eliminate(wide)
    return pltpu.roll(done, LANES - n, 1)[:, 0:n]


def dot_nn(a, b):
    return jnp.dot(a, b, precision=HIGHEST, preferred_element_type=F32)


def last_kernel(count, scale, locked_ref, *refs):
    messages = refs[:count]
    x_ref, ax_ref, a2x_ref, w_ref, wi_ref, ritz_ref = refs[count:]
    k = x_ref.shape[0]
    locked = locked_ref[0]
    total, q = merged([r[...] for r in messages], k)
    total = total * scale
    plain = total[:, 0 : 3 * k]
    image = pltpu.roll(total, LANES - 3 * k, 1)[:, 0 : 3 * k]
    row = iota2((k, k), 0)
    col = iota2((k, k), 1)
    active = (row >= locked) & (col >= locked)
    frozen = (row == col) & (row < locked)
    residual_gram = pltpu.roll(total, LANES - k, 1)[k : 2 * k, 0:k]
    gram_w = jnp.where(active, residual_gram, 0.0) + jnp.where(frozen, 1.0, 0.0)
    inverse_w = jnp.where(active, inverse_factor(gram_w), 0.0)
    residual = ax_ref[...] - q * x_ref[...]
    w_ref[...] = dot_nn(inverse_w, residual)
    wi_ref[...] = dot_nn(inverse_w, a2x_ref[...] - q * ax_ref[...])
    zeros = jnp.zeros((k, LANES - k), F32)
    mid = pltpu.roll(jnp.concatenate([inverse_w, zeros], axis=1), k, 1)[:, 0 : 3 * k]
    row3 = iota2((3 * k, 3 * k), 0)
    col3 = iota2((3 * k, 3 * k), 1)
    same = row3 == col3
    middle = (row3 >= k) & (row3 < 2 * k)
    empty = jnp.zeros((k, 3 * k), F32)
    change = jnp.where(same & ~middle, 1.0, jnp.concatenate([empty, mid, empty], axis=0))
    gram_b = dot_nt(dot_nn(change, plain), change)
    pad = same & (row3 >= k) & (row3 < k + locked)
    gram_b = gram_b + jnp.where(pad, 1.0, 0.0)
    gram_a = dot_nt(dot_nn(change, image), change)
    symmetric = 0.5 * (gram_a + gram_a.T)
    inverse_b = inverse_factor(gram_b)
    ritz_ref[...] = dot_nt(dot_nn(inverse_b, symmetric), inverse_b)


def stages(members):
    found, stride = [], 1
    while stride < members:
        size = 4 if stride * 4 <= members else 2
        found.append((stride, size))
        stride *= size
    assert stride == members
    return found


def body(current_block, previous_block, adjacency_tiles, tile_rows, tile_cols, tile_count, locked):
    k, rows_here = current_block.shape
    slots, tile, _ = adjacency_tiles.shape
    members = lax.axis_size(AXES)
    vertex_total = rows_here * members
    row_tiles = rows_here // tile
    reach = row_tiles // 2
    width = reach * tile
    span = row_tiles + 2 * reach
    up = [(i, i + 1) for i in range(members - 1)]
    down = [(i + 1, i) for i in range(members - 1)]

    def halo(head, tail):
        return lax.ppermute(tail, AXES, up), lax.ppermute(head, AXES, down)

    def sds(*shape):
        return jax.ShapeDtypeStruct(shape, F32)

    left, right = halo(current_block[:, :width], current_block[:, rows_here - width :])
    pleft, pright = halo(previous_block[:, :width], previous_block[:, rows_here - width :])
    x_image, head, tail = pl.pallas_call(
        functools.partial(first_kernel, tile),
        out_shape=(sds(k, rows_here), sds(k, width), sds(k, width)),
        in_specs=[SMEM] * 3 + [VMEM] * 4,
        out_specs=(VMEM,) * 3,
        scratch_shapes=[
            pltpu.VMEM((span, 3 * k, tile), BF16),
            pltpu.VMEM((row_tiles, k, tile), F32),
        ],
        name="first_apply",
    )(tile_rows, tile_cols, tile_count, current_block, left, right, adjacency_tiles)
    aleft, aright = halo(head, tail)
    twice, message = pl.pallas_call(
        functools.partial(second_kernel, tile),
        out_shape=(sds(k, rows_here), sds(3 * k, LANES)),
        in_specs=[SMEM] * 3 + [VMEM] * 8,
        out_specs=(VMEM,) * 2,
        scratch_shapes=[
            pltpu.VMEM((span, 6 * k, tile), BF16),
            pltpu.VMEM((row_tiles, 2 * k, tile), F32),
            pltpu.VMEM((6 * k, rows_here), F32),
        ],
        name="second_apply",
    )(tile_rows, tile_cols, tile_count, current_block, previous_block, pleft, pright,
      x_image, aleft, aright, adjacency_tiles)
    plan = stages(members)
    for number, (stride, size) in enumerate(plan):
        messages = [message] + [
            lax.ppermute(message, AXES, [(i, i ^ (m * stride)) for i in range(members)])
            for m in range(1, size)
        ]
        if number < len(plan) - 1:
            message = pl.pallas_call(
                merge_kernel,
                out_shape=sds(3 * k, LANES),
                in_specs=[VMEM] * size,
                out_specs=VMEM,
                name="merge",
            )(*messages)
    return pl.pallas_call(
        functools.partial(last_kernel, len(messages), 1.0 / vertex_total),
        out_shape=(sds(k, rows_here), sds(k, rows_here), sds(3 * k, 3 * k)),
        in_specs=[SMEM] + [VMEM] * (len(messages) + 3),
        out_specs=(VMEM,) * 3,
        name="finish",
    )(locked, *messages, current_block, x_image, twice)


def solution(mesh):
    in_specs = (
        P(None, ("graphs", "rows", "cols", "sub")),
        P(None, ("graphs", "rows", "cols", "sub")),
        P(("graphs", "rows", "cols", "sub"), None, None),
        P(("graphs", "rows", "cols", "sub")),
        P(("graphs", "rows", "cols", "sub")),
        P(("graphs", "rows", "cols", "sub")),
        P("graphs"),
    )
    out_specs = (
        P(None, ("graphs", "rows", "cols", "sub")),
        P(None, ("graphs", "rows", "cols", "sub")),
        P("graphs", None),
    )
    return jax.shard_map(body, mesh=mesh, in_specs=in_specs, out_specs=out_specs, check_vma=False)
```

time: 183 us -> 63.6 us (0.35)
  blocking collectives: 126 us -> 0 us
  Pallas kernels: 0 us -> 21.3 us
  other arithmetic: 21 us -> 0 us
  starting transfers between devices: 7.44 us -> 26.1 us
  matrix products: 16.3 us -> 0 us
  waiting for transfers between devices: 0.01 us -> 8.21 us
  local copies, waits for them, and re-layouts: 9.1 us -> 5.44 us
    psum x3 -> x0, blocking collectives: 126 us -> none  [the longest x1 60.5 us: body(): lax.psum((inner_products(search, search), inner_products(search, search_i...]
    pallas_call x0 -> x4, Pallas kernels: none -> 21.3 us  [the longest x1 8.71 us: body(): pl.pallas_call(functools.partial(last_kernel, len(messages), 1.0 / vertex...]
    ppermute x4 -> x12, starting transfers between devices: 7.44 us -> 26.1 us  [the longest x6 15.7 us: halo(): return (lax.ppermute(tail, AXES, up), lax.ppermute(head, AXES, down))]
    dot_general x7 -> x0, matrix products: 14 us -> none  [the longest x2 7.77 us: operate(): jnp.einsum('cta,tab->ctb', gathered, adjacency_tiles, precision=lax.Preci...]
    another operation x10 -> x0, other arithmetic: 13.4 us -> none  [the longest x4 6.2 us: solve_lower(): lax.linalg.triangular_solve(factor, values, left_side=True, lower=True)]
    ppermute x4 -> x12, waiting for transfers between devices: 0.01 us -> 8.21 us  [the longest x6 5.96 us: body(): lax.ppermute(message, AXES, [(i, i ^ m * stride) for i in range(members)])]
    gather x2 -> x0, local copies, waits for them, and re-layouts: 4.78 us -> none  [operate(): gathered = jnp.take(column_blocks, column_position, axis=1)]
    reshape x2 -> x0, other arithmetic: 2.55 us -> none  [operate(): column_blocks = padded.reshape(channels, span_tiles, tile_size)]
  transfers between devices with their start and end apart: 4 -> 12, of which waited for: 0 -> 6; matrix products, arithmetic and copies ran while one was open for 2% -> 1% of each run, Pallas kernels for 0% -> 8%
where the time goes in v1:
time: 63.6 us; the launch traced here: 63.2 us
  starting transfers between devices  26.1 us (41%)
  Pallas kernels  21.3 us (33%)
  waiting for transfers between devices  8.21 us (13%)
  local copies, waits for them, and re-layouts  5.44 us (9%)
  between operations  2.08 us (3%)
    ppermute x6, starting transfers between devices, halo(): return (lax.ppermute(tail, AXES, up), lax.ppermute(head, AXES, down))  15.7 us
    ppermute x6, starting transfers between devices, body(): lax.ppermute(message, AXES, [(i, i ^ m * stride) for i in range(members)])  10.5 us
    pallas_call x1, Pallas kernels, body(): pl.pallas_call(functools.partial(last_kernel, len(messages), 1.0 / vertex...  8.71 us
    pallas_call x1, Pallas kernels, body(): pl.pallas_call(functools.partial(second_kernel, tile), out_shape=(sds(k,...  6.16 us
    ppermute x6, waiting for transfers between devices, body(): lax.ppermute(message, AXES, [(i, i ^ m * stride) for i in range(members)])  5.96 us
    pallas_call x1, Pallas kernels, body(): pl.pallas_call(functools.partial(first_kernel, tile), out_shape=(sds(k, r...  4.84 us
    unnamed x24, local copies, waits for them, and re-layouts  3.67 us
    ppermute x6, waiting for transfers between devices, halo(): return (lax.ppermute(tail, AXES, up), lax.ppermute(head, AXES, down))  2.25 us
  transfers between devices with their start and end apart: 12, of which 6 were waited for; matrix products, arithmetic and copies ran while one was open for 1% of the time, Pallas kernels for 8%

profile of v1, /device:TPU:0, one launch (start us, length us, event | category | flops | bytes accessed | tf_op | source)
XLA Modules:
  0.0 63.2 jit_solution(10912955347992313501)
XLA Ops:
  0.6 0.9 %fusion = (f32[16,1024]{1,0:T(8,128)S(1)}, f32[16,1024]{1,0:T(8,128)S(1)}) fusion(f32[16,2048]{1,0:T(8,128)} %refs_4_.1), kind=kLoop, calls=%fused_computation | loop fusion | bytes 262144 | tf_op jit(solution)/shard_map/slice | solution.py:271
  1.5 1.3 %collective-permute-start.3 = (f32[16,1024]{1,0:T(8,128)S(1)}, f32[16,1024]{1,0:T(8,128)S(1)}, u32[]{:S(2)}, u32[]{:S(2)}) collective-permute-start(f32[16,1024]{1,0:T(8,128)S(1)} %get-tuple-element.13), channel_id=1, source_target_pairs={{1,0},{2,1},{3,2},{4,3},{5,4},{6,5},{7,6},{8,7},{9,8},{10,9},{11,1... | collective-permute-start | bytes 196616 | tf_op jit(solution)/shard_map/ppermute | solution.py:266
  2.8 3.0 %collective-permute-start.2 = (f32[16,1024]{1,0:T(8,128)S(1)}, f32[16,1024]{1,0:T(8,128)S(1)}, u32[]{:S(2)}, u32[]{:S(2)}) collective-permute-start(f32[16,1024]{1,0:T(8,128)S(1)} %get-tuple-element.14), channel_id=1, source_target_pairs={{0,1},{1,2},{2,3},{3,4},{4,5},{5,6},{6,7},{7,8},{8,9},{9,10},{10,1... | collective-permute-start | bytes 196616 | tf_op jit(solution)/shard_map/ppermute | solution.py:266
  5.9 0.9 %fusion.1 = (f32[16,1024]{1,0:T(8,128)S(1)}, f32[16,1024]{1,0:T(8,128)S(1)}) fusion(f32[16,2048]{1,0:T(8,128)} %p_ref.1), kind=kLoop, calls=%fused_computation.1 | loop fusion | bytes 262144 | tf_op jit(solution)/shard_map/slice | solution.py:272
  6.7 1.3 %collective-permute-start.1 = (f32[16,1024]{1,0:T(8,128)S(1)}, f32[16,1024]{1,0:T(8,128)S(1)}, u32[]{:S(2)}, u32[]{:S(2)}) collective-permute-start(f32[16,1024]{1,0:T(8,128)S(1)} %get-tuple-element.15), channel_id=1, source_target_pairs={{1,0},{2,1},{3,2},{4,3},{5,4},{6,5},{7,6},{8,7},{9,8},{10,9},{11,1... | collective-permute-start | bytes 196616 | tf_op jit(solution)/shard_map/ppermute | solution.py:266
  8.0 5.1 %collective-permute-start = (f32[16,1024]{1,0:T(8,128)S(1)}, f32[16,1024]{1,0:T(8,128)S(1)}, u32[]{:S(2)}, u32[]{:S(2)}) collective-permute-start(f32[16,1024]{1,0:T(8,128)S(1)} %get-tuple-element.16), channel_id=1, source_target_pairs={{0,1},{1,2},{2,3},{3,4},{4,5},{5,6},{6,7},{7,8},{8,9},{9,10},{10,1... | collective-permute-start | bytes 196616 | tf_op jit(solution)/shard_map/ppermute | solution.py:266
  13.9 0.6 copy-done.4
  14.5 0.6 copy-done.5
  15.1 4.8 %first_apply.1 = (f32[16,2048]{1,0:T(8,128)}, f32[16,1024]{1,0:T(8,128)}, f32[16,1024]{1,0:T(8,128)}) custom-call(s32[48]{0:T(128)} %rows_ref.3, s32[48]{0:T(128)} %cols_ref.3, s32[1]{0:T(128)S(6)} %copy.10.count_ref, f32[16,2048]{1,0:T(8,128)} %refs_4_.1, f32[16,1024]{1,0:T(8,128)} %copy-done.5, f32[16,1024]{1,0:T(8,128)} %copy-done.4, ...), custom_call_target="tpu_custom_call" | custom-call | tf_op jit(solution)/shard_map/first_apply/pallas_call | solution.py:273
  19.9 3.6 %collective-permute-start.4 = (f32[16,1024]{1,0:T(8,128)}, f32[16,1024]{1,0:T(8,128)S(1)}, u32[]{:S(2)}, u32[]{:S(2)}) collective-permute-start(f32[16,1024]{1,0:T(8,128)} %get-tuple-element.9), channel_id=1, source_target_pairs={{0,1},{1,2},{2,3},{3,4},{4,5},{5,6},{6,7},{7,8},{8,9},{9,10},{10,1... | collective-permute-start | bytes 196616 | tf_op jit(solution)/shard_map/ppermute | solution.py:266
  23.6 1.3 %collective-permute-start.5 = (f32[16,1024]{1,0:T(8,128)}, f32[16,1024]{1,0:T(8,128)S(1)}, u32[]{:S(2)}, u32[]{:S(2)}) collective-permute-start(f32[16,1024]{1,0:T(8,128)} %get-tuple-element.10), channel_id=1, source_target_pairs={{1,0},{2,1},{3,2},{4,3},{5,4},{6,5},{7,6},{8,7},{9,8},{10,9},{11,1... | collective-permute-start | bytes 196616 | tf_op jit(solution)/shard_map/ppermute | solution.py:266
  24.9 2.2 %collective-permute-done.5.aright_ref = f32[16,1024]{1,0:T(8,128)S(1)} collective-permute-done((f32[16,1024]{1,0:T(8,128)}, f32[16,1024]{1,0:T(8,128)S(1)}, u32[]{:S(2)}, u32[]{:S(2)}) %collective-permute-start.5) | collective-permute-done | bytes 65568 | tf_op jit(solution)/shard_map/ppermute | solution.py:266
  27.8 6.2 %second_apply.1 = (f32[16,2048]{1,0:T(8,128)}, f32[48,128]{1,0:T(8,128)}) custom-call(s32[48]{0:T(128)} %rows_ref.3, s32[48]{0:T(128)} %cols_ref.3, s32[1]{0:T(128)S(6)} %copy.10.count_ref, f32[16,2048]{1,0:T(8,128)} %refs_4_.1, f32[16,2048]{1,0:T(8,128)} %p_ref.1, f32[16,1024]{1,0:T(8,128)} %copy-done.1, f32[16,1024]{1,0:T(8,128)} %copy-done, ...), custom_call_target="tpu_custom_call" | custom-call | tf_op jit(solution)/shard_map/second_apply/pallas_call | solution.py:285
  34.0 6.0 %collective-permute-start.8 = (f32[48,128]{1,0:T(8,128)}, f32[48,128]{1,0:T(8,128)S(1)}, u32[]{:S(2)}, u32[]{:S(2)}) collective-permute-start(f32[48,128]{1,0:T(8,128)} %get-tuple-element.11.refs_0_), channel_id=1, source_target_pairs={{0,3},{1,2},{2,1},{3,0},{4,7},{5,6},{6,5},{7,4},{8,11},{9,10},{10,... | collective-permute-start | bytes 73736 | tf_op jit(solution)/shard_map/ppermute | solution.py:301
  40.0 1.7 %collective-permute-done.8.refs_3_ = f32[48,128]{1,0:T(8,128)S(1)} collective-permute-done((f32[48,128]{1,0:T(8,128)}, f32[48,128]{1,0:T(8,128)S(1)}, u32[]{:S(2)}, u32[]{:S(2)}) %collective-permute-start.8) | collective-permute-done | bytes 24608 | tf_op jit(solution)/shard_map/ppermute | solution.py:301
  41.7 2.3 %collective-permute-done.7.refs_2_ = f32[48,128]{1,0:T(8,128)S(1)} collective-permute-done((f32[48,128]{1,0:T(8,128)}, f32[48,128]{1,0:T(8,128)S(1)}, u32[]{:S(2)}, u32[]{:S(2)}) %collective-permute-start.7) | collective-permute-done | bytes 24608 | tf_op jit(solution)/shard_map/ppermute | solution.py:301
  44.6 0.6 copy-done.11
  45.2 1.6 %merge.1.refs_0_ = f32[48,128]{1,0:T(8,128)} custom-call(f32[48,128]{1,0:T(8,128)} %get-tuple-element.11.refs_0_, f32[48,128]{1,0:T(8,128)} %copy-done.11, f32[48,128]{1,0:T(8,128)} %copy-done.10, f32[48,128]{1,0:T(8,128)} %copy-done.9), custom_call_target="tpu_custom_call" | custom-call | tf_op jit(solution)/shard_map/merge/pallas_call | solution.py:305
  46.8 0.9 %collective-permute-start.11 = (f32[48,128]{1,0:T(8,128)}, f32[48,128]{1,0:T(8,128)S(1)}, u32[]{:S(2)}, u32[]{:S(2)}) collective-permute-start(f32[48,128]{1,0:T(8,128)} %merge.1.refs_0_), channel_id=1, source_target_pairs={{0,12},{1,13},{2,14},{3,15},{4,8},{5,9},{6,10},{7,11},{8,4},{9,5},... | collective-permute-start | bytes 73736 | tf_op jit(solution)/shard_map/ppermute | solution.py:301
  47.7 2.1 %collective-permute-start.10 = (f32[48,128]{1,0:T(8,128)}, f32[48,128]{1,0:T(8,128)S(1)}, u32[]{:S(2)}, u32[]{:S(2)}) collective-permute-start(f32[48,128]{1,0:T(8,128)} %merge.1.refs_0_), channel_id=1, source_target_pairs={{0,8},{1,9},{2,10},{3,11},{4,12},{5,13},{6,14},{7,15},{8,0},{9,1},... | collective-permute-start | bytes 73736 | tf_op jit(solution)/shard_map/ppermute | solution.py:301
  49.8 1.3 %collective-permute-start.9 = (f32[48,128]{1,0:T(8,128)}, f32[48,128]{1,0:T(8,128)S(1)}, u32[]{:S(2)}, u32[]{:S(2)}) collective-permute-start(f32[48,128]{1,0:T(8,128)} %merge.1.refs_0_), channel_id=1, source_target_pairs={{0,4},{1,5},{2,6},{3,7},{4,0},{5,1},{6,2},{7,3},{8,12},{9,13},{10,... | collective-permute-start | bytes 73736 | tf_op jit(solution)/shard_map/ppermute | solution.py:301
  51.8 0.8 %collective-permute-done.11.refs_3_ = f32[48,128]{1,0:T(8,128)S(1)} collective-permute-done((f32[48,128]{1,0:T(8,128)}, f32[48,128]{1,0:T(8,128)S(1)}, u32[]{:S(2)}, u32[]{:S(2)}) %collective-permute-start.11) | collective-permute-done | bytes 24608 | tf_op jit(solution)/shard_map/ppermute | solution.py:301
  52.9 1.0 %collective-permute-done.9.refs_1_ = f32[48,128]{1,0:T(8,128)S(1)} collective-permute-done((f32[48,128]{1,0:T(8,128)}, f32[48,128]{1,0:T(8,128)S(1)}, u32[]{:S(2)}, u32[]{:S(2)}) %collective-permute-start.9) | collective-permute-done | bytes 24608 | tf_op jit(solution)/shard_map/ppermute | solution.py:301
  54.4 8.7 %finish.1 = (f32[16,2048]{1,0:T(8,128)}, f32[16,2048]{1,0:T(8,128)}, f32[48,48]{1,0:T(8,128)}) custom-call(s32[1]{0:T(128)S(6)} %copy.11.locked_ref, f32[48,128]{1,0:T(8,128)} %merge.1.refs_0_, f32[48,128]{1,0:T(8,128)} %copy-done.8, f32[48,128]{1,0:T(8,128)} %copy-done.7, f32[48,128]{1,0:T(8,128)} %copy-done.6, f32[16,2048]{1,0:T(8,128)} %refs_4_.1, ...), custom_call_target="tpu_custom_call" | custom-call | tf_op jit(solution)/shard_map/finish/pallas_call | solution.py:312
  (30 shorter events, 2.2 us)
Async XLA Ops:
  1.5 12.3 %collective-permute-start.3 = (f32[16,1024]{1,0:T(8,128)S(1)}, f32[16,1024]{1,0:T(8,128)S(1)}, u32[]{:S(2)}, u32[]{:S(2)}) collective-permute-start(f32[16,1024]{1,0:T(8,128)S(1)} %get-tuple-element.13), channel_id=1, source_target_pairs={{1,0},{2,1},{3,2},{4,3},{5,4},{6,5},{7,6},{8,7},{9,8},{10,9},{11,1... | collective-permute-start | bytes 196616 | tf_op jit(solution)/shard_map/ppermute | solution.py:266
  2.8 11.0 %collective-permute-start.2 = (f32[16,1024]{1,0:T(8,128)S(1)}, f32[16,1024]{1,0:T(8,128)S(1)}, u32[]{:S(2)}, u32[]{:S(2)}) collective-permute-start(f32[16,1024]{1,0:T(8,128)S(1)} %get-tuple-element.14), channel_id=1, source_target_pairs={{0,1},{1,2},{2,3},{3,4},{4,5},{5,6},{6,7},{7,8},{8,9},{9,10},{10,1... | collective-permute-start | bytes 196616 | tf_op jit(solution)/shard_map/ppermute | solution.py:266
  6.7 18.1 %collective-permute-start.1 = (f32[16,1024]{1,0:T(8,128)S(1)}, f32[16,1024]{1,0:T(8,128)S(1)}, u32[]{:S(2)}, u32[]{:S(2)}) collective-permute-start(f32[16,1024]{1,0:T(8,128)S(1)} %get-tuple-element.15), channel_id=1, source_target_pairs={{1,0},{2,1},{3,2},{4,3},{5,4},{6,5},{7,6},{8,7},{9,8},{10,9},{11,1... | collective-permute-start | bytes 196616 | tf_op jit(solution)/shard_map/ppermute | solution.py:266
  8.0 16.9 %collective-permute-start = (f32[16,1024]{1,0:T(8,128)S(1)}, f32[16,1024]{1,0:T(8,128)S(1)}, u32[]{:S(2)}, u32[]{:S(2)}) collective-permute-start(f32[16,1024]{1,0:T(8,128)S(1)} %get-tuple-element.16), channel_id=1, source_target_pairs={{0,1},{1,2},{2,3},{3,4},{4,5},{5,6},{6,7},{7,8},{8,9},{9,10},{10,1... | collective-permute-start | bytes 196616 | tf_op jit(solution)/shard_map/ppermute | solution.py:266
  13.8 0.6 %copy-start.4 = (f32[16,1024]{1,0:T(8,128)}, f32[16,1024]{1,0:T(8,128)S(1)}, u32[]{:S(2)}) copy-start(f32[16,1024]{1,0:T(8,128)S(1)} %collective-permute-done.3.right_ref) | copy-start | bytes 196612
  14.5 0.6 copy-start.5
  19.9 5.0 %collective-permute-start.4 = (f32[16,1024]{1,0:T(8,128)}, f32[16,1024]{1,0:T(8,128)S(1)}, u32[]{:S(2)}, u32[]{:S(2)}) collective-permute-start(f32[16,1024]{1,0:T(8,128)} %get-tuple-element.9), channel_id=1, source_target_pairs={{0,1},{1,2},{2,3},{3,4},{4,5},{5,6},{6,7},{7,8},{8,9},{9,10},{10,1... | collective-permute-start | bytes 196616 | tf_op jit(solution)/shard_map/ppermute | solution.py:266
  23.6 3.6 %collective-permute-start.5 = (f32[16,1024]{1,0:T(8,128)}, f32[16,1024]{1,0:T(8,128)S(1)}, u32[]{:S(2)}, u32[]{:S(2)}) collective-permute-start(f32[16,1024]{1,0:T(8,128)} %get-tuple-element.10), channel_id=1, source_target_pairs={{1,0},{2,1},{3,2},{4,3},{5,4},{6,5},{7,6},{8,7},{9,8},{10,9},{11,1... | collective-permute-start | bytes 196616 | tf_op jit(solution)/shard_map/ppermute | solution.py:266
  24.9 2.3 %copy-start = (f32[16,1024]{1,0:T(8,128)}, f32[16,1024]{1,0:T(8,128)S(1)}, u32[]{:S(2)}) copy-start(f32[16,1024]{1,0:T(8,128)S(1)} %collective-permute-done.1.pright_ref) | copy-start | bytes 196612
  24.9 2.3 %copy-start.1 = (f32[16,1024]{1,0:T(8,128)}, f32[16,1024]{1,0:T(8,128)S(1)}, u32[]{:S(2)}) copy-start(f32[16,1024]{1,0:T(8,128)S(1)} %collective-permute-done.pleft_ref) | copy-start | bytes 196612
  24.9 2.3 %copy-start.2 = (f32[16,1024]{1,0:T(8,128)}, f32[16,1024]{1,0:T(8,128)S(1)}, u32[]{:S(2)}) copy-start(f32[16,1024]{1,0:T(8,128)S(1)} %collective-permute-done.4.aleft_ref) | copy-start | bytes 196612
  27.2 0.6 copy-start.3
  34.0 7.7 %collective-permute-start.8 = (f32[48,128]{1,0:T(8,128)}, f32[48,128]{1,0:T(8,128)S(1)}, u32[]{:S(2)}, u32[]{:S(2)}) collective-permute-start(f32[48,128]{1,0:T(8,128)} %get-tuple-element.11.refs_0_), channel_id=1, source_target_pairs={{0,3},{1,2},{2,1},{3,0},{4,7},{5,6},{6,5},{7,4},{8,11},{9,10},{10,... | collective-permute-start | bytes 73736 | tf_op jit(solution)/shard_map/ppermute | solution.py:301
  39.9 4.0 %collective-permute-start.7 = (f32[48,128]{1,0:T(8,128)}, f32[48,128]{1,0:T(8,128)S(1)}, u32[]{:S(2)}, u32[]{:S(2)}) collective-permute-start(f32[48,128]{1,0:T(8,128)} %get-tuple-element.11.refs_0_), channel_id=1, source_target_pairs={{0,2},{1,3},{2,0},{3,1},{4,6},{5,7},{6,4},{7,5},{8,10},{9,11},{10,... | collective-permute-start | bytes 73736 | tf_op jit(solution)/shard_map/ppermute | solution.py:301
  39.9 4.0 %collective-permute-start.6 = (f32[48,128]{1,0:T(8,128)}, f32[48,128]{1,0:T(8,128)S(1)}, u32[]{:S(2)}, u32[]{:S(2)}) collective-permute-start(f32[48,128]{1,0:T(8,128)} %get-tuple-element.11.refs_0_), channel_id=1, source_target_pairs={{0,1},{1,0},{2,3},{3,2},{4,5},{5,4},{6,7},{7,6},{8,9},{9,8},{10,11... | collective-permute-start | bytes 73736 | tf_op jit(solution)/shard_map/ppermute | solution.py:301
  41.7 2.3 %copy-start.9 = (f32[48,128]{1,0:T(8,128)}, f32[48,128]{1,0:T(8,128)S(1)}, u32[]{:S(2)}) copy-start(f32[48,128]{1,0:T(8,128)S(1)} %collective-permute-done.8.refs_3_) | copy-start | bytes 73732
  43.9 0.6 copy-start.10
  44.6 0.6 copy-start.11
  46.8 5.9 %collective-permute-start.11 = (f32[48,128]{1,0:T(8,128)}, f32[48,128]{1,0:T(8,128)S(1)}, u32[]{:S(2)}, u32[]{:S(2)}) collective-permute-start(f32[48,128]{1,0:T(8,128)} %merge.1.refs_0_), channel_id=1, source_target_pairs={{0,12},{1,13},{2,14},{3,15},{4,8},{5,9},{6,10},{7,11},{8,4},{9,5},... | collective-permute-start | bytes 73736 | tf_op jit(solution)/shard_map/ppermute | solution.py:301
  47.7 5.2 %collective-permute-start.10 = (f32[48,128]{1,0:T(8,128)}, f32[48,128]{1,0:T(8,128)S(1)}, u32[]{:S(2)}, u32[]{:S(2)}) collective-permute-start(f32[48,128]{1,0:T(8,128)} %merge.1.refs_0_), channel_id=1, source_target_pairs={{0,8},{1,9},{2,10},{3,11},{4,12},{5,13},{6,14},{7,15},{8,0},{9,1},... | collective-permute-start | bytes 73736 | tf_op jit(solution)/shard_map/ppermute | solution.py:301
  49.8 4.0 %collective-permute-start.9 = (f32[48,128]{1,0:T(8,128)}, f32[48,128]{1,0:T(8,128)S(1)}, u32[]{:S(2)}, u32[]{:S(2)}) collective-permute-start(f32[48,128]{1,0:T(8,128)} %merge.1.refs_0_), channel_id=1, source_target_pairs={{0,4},{1,5},{2,6},{3,7},{4,0},{5,1},{6,2},{7,3},{8,12},{9,13},{10,... | collective-permute-start | bytes 73736 | tf_op jit(solution)/shard_map/ppermute | solution.py:301
  52.6 1.2 %copy-start.6 = (f32[48,128]{1,0:T(8,128)}, f32[48,128]{1,0:T(8,128)S(1)}, u32[]{:S(2)}) copy-start(f32[48,128]{1,0:T(8,128)S(1)} %collective-permute-done.11.refs_3_) | copy-start | bytes 73732
  52.9 1.0 %copy-start.7 = (f32[48,128]{1,0:T(8,128)}, f32[48,128]{1,0:T(8,128)S(1)}, u32[]{:S(2)}) copy-start(f32[48,128]{1,0:T(8,128)S(1)} %collective-permute-done.10.refs_2_) | copy-start | bytes 73732
  53.8 0.6 copy-start.8

commit v2 on v1

--- a/solution.py
+++ b/solution.py
@@ -13,6 +13,8 @@
 HIGHEST = lax.Precision.HIGHEST
 LANES = 128
 UNROLL = 8
+GROUP = 4
+VMEM_LIMIT = 24 * 1024 * 1024
 VMEM = pl.BlockSpec(memory_space=pltpu.VMEM)
 SMEM = pl.BlockSpec(memory_space=pltpu.SMEM)
 
@@ -44,7 +46,7 @@
 
 def tile_product(parts_ref, tiles_ref, t, col, height):
     lhs = parts_ref[col]
-    t1, t2, t3 = split3(tiles_ref[t])
+    t1, t2, t3 = tiles_ref[0, t], tiles_ref[1, t], tiles_ref[2, t]
     y1 = jnp.dot(lhs, t1, preferred_element_type=F32)
     y2 = jnp.dot(lhs[: 2 * height], t2, preferred_element_type=F32)
     y3 = jnp.dot(lhs[:height], t3, preferred_element_type=F32)
@@ -52,11 +54,11 @@
     return y1[:h] + ((y1[h : 2 * h] + y2[:h]) + (y1[2 * h :] + y2[h : 2 * h] + y3))
 
 
-def apply_tiles(parts_ref, sums_ref, tiles_ref, rows_ref, cols_ref, count_ref, height, reach):
+def apply_tiles(parts_ref, sums_ref, tiles_ref, meta_ref, height, reach):
     row_tiles = sums_ref.shape[0]
-    slots = tiles_ref.shape[0]
-    base = rows_ref[0]
-    count = count_ref[0]
+    slots = tiles_ref.shape[1]
+    base = meta_ref[0]
+    count = meta_ref[2 * slots]
 
     def diagonal(step, carry):
         for u in range(UNROLL):
@@ -70,8 +72,8 @@
         found = []
         for u in range(UNROLL):
             t = row_tiles + step * UNROLL + u
-            y = tile_product(parts_ref, tiles_ref, t, cols_ref[t] - base + reach, height)
-            found.append((rows_ref[t] - base, jnp.where(t < count, y, 0.0)))
+            y = tile_product(parts_ref, tiles_ref, t, meta_ref[slots + t] - base + reach, height)
+            found.append((meta_ref[t] - base, jnp.where(t < count, y, 0.0)))
         for row, y in found:
             sums_ref[row] += y
         return carry
@@ -79,13 +81,23 @@
     lax.fori_loop(0, (slots - row_tiles) // UNROLL, extra, 0)
 
 
-def first_kernel(tile, rows_ref, cols_ref, count_ref, x_ref, left_ref, right_ref, tiles_ref,
+def split_kernel(tiles_ref, out_ref):
+    def step(t, carry):
+        for u in range(2):
+            for k, part in enumerate(split3(tiles_ref[2 * t + u])):
+                out_ref[k, 2 * t + u] = part
+        return carry
+
+    lax.fori_loop(0, tiles_ref.shape[0] // 2, step, 0)
+
+
+def first_kernel(tile, meta_ref, x_ref, left_ref, right_ref, tiles_ref,
                  image_ref, head_ref, tail_ref, parts_ref, sums_ref):
     channels = x_ref.shape[0]
     reach = left_ref.shape[1] // tile
     row_tiles = sums_ref.shape[0]
-    load_span(parts_ref, 0, channels, left_ref, x_ref, right_ref, tile)
-    apply_tiles(parts_ref, sums_ref, tiles_ref, rows_ref, cols_ref, count_ref, channels, reach)
+    load_span(parts_ref, 0, channels, left_ref.at[0:channels], x_ref, right_ref.at[0:channels], tile)
+    apply_tiles(parts_ref, sums_ref, tiles_ref, meta_ref, channels, reach)
     for i in range(row_tiles):
         cut = slice(i * tile, (i + 1) * tile)
         value = x_ref[:, cut] - sums_ref[i]
@@ -106,15 +118,15 @@
                            preferred_element_type=F32)
 
 
-def second_kernel(tile, rows_ref, cols_ref, count_ref, x_ref, p_ref, pleft_ref, pright_ref,
+def second_kernel(tile, meta_ref, x_ref, p_ref, pleft_ref, pright_ref,
                   ax_ref, aleft_ref, aright_ref, tiles_ref, a2x_ref, message_ref,
                   parts_ref, sums_ref, basis_ref):
     k = x_ref.shape[0]
     reach = aleft_ref.shape[1] // tile
     row_tiles = sums_ref.shape[0]
-    load_span(parts_ref, k, 2 * k, pleft_ref, p_ref, pright_ref, tile)
+    load_span(parts_ref, k, 2 * k, pleft_ref.at[k : 2 * k], p_ref, pright_ref.at[k : 2 * k], tile)
     load_span(parts_ref, 0, 2 * k, aleft_ref, ax_ref, aright_ref, tile)
-    apply_tiles(parts_ref, sums_ref, tiles_ref, rows_ref, cols_ref, count_ref, 2 * k, reach)
+    apply_tiles(parts_ref, sums_ref, tiles_ref, meta_ref, 2 * k, reach)
     x = x_ref[...]
     ax = ax_ref[...]
     q = jnp.sum(x * ax, axis=1, keepdims=True) / (jnp.sum(x * x, axis=1, keepdims=True) + 1e-06)
@@ -175,19 +187,37 @@
 
 def eliminate(matrix):
     n = matrix.shape[0]
+    full = (8, LANES)
     blocks = [matrix[b : b + 8] for b in range(0, n, 8)]
-    sub = iota2((8, LANES), 0)
-    for j in range(n):
-        b0, r0 = divmod(j, 8)
-        line = blocks[b0][r0 : r0 + 1]
-        pivot = line[:, j : j + 1]
-        root = lax.rsqrt(pivot)
-        root = root * (1.5 - 0.5 * pivot * root * root)
-        line = line * root
-        for b in range(b0, len(blocks)):
-            update = blocks[b] - (blocks[b][:, j : j + 1] * root) * line
+    sub = iota2(full, 0)
+    for g in range(0, n, GROUP):
+        b0, r0 = divmod(g, 8)
+        rows = [jnp.broadcast_to(blocks[b0][r0 + i : r0 + i + 1], full) for i in range(GROUP)]
+        s = [[jnp.broadcast_to(rows[i][:, g + l : g + l + 1], full) if l >= i else None
+              for l in range(GROUP)] for i in range(GROUP)]
+        cols = {b: [jnp.broadcast_to(blocks[b][:, g + i : g + i + 1], full) for i in range(GROUP)]
+                for b in range(b0, len(blocks))}
+        for a in range(GROUP):
+            inverse = 1.0 / s[a][a]
+            for l in range(a + 1, GROUP):
+                f = s[a][l] * inverse
+                for c in range(l, GROUP):
+                    s[l][c] = s[l][c] - f * s[a][c]
+                rows[l] = rows[l] - f * rows[a]
+                for b in cols:
+                    cols[b][l] = cols[b][l] - f * cols[b][a]
+            for b in cols:
+                cols[b][a] = cols[b][a] * inverse
+        for b in cols:
+            update = blocks[b]
+            for a in range(GROUP):
+                update = update - cols[b][a] * rows[a]
             if b == b0:
-                update = jnp.where(sub > r0, update, jnp.where(sub == r0, line, blocks[b]))
+                update = jnp.where(sub >= r0 + GROUP, update, blocks[b])
+                for a in range(GROUP):
+                    root = lax.rsqrt(s[a][a])
+                    root = root * (1.5 - 0.5 * s[a][a] * root * root)
+                    update = jnp.where(sub == r0 + a, rows[a] * root, update)
             blocks[b] = update
     return jnp.concatenate(blocks, axis=0)
 
@@ -243,7 +273,7 @@
 def stages(members):
     found, stride = [], 1
     while stride < members:
-        size = 4 if stride * 4 <= members else 2
+        size = 2
         found.append((stride, size))
         stride *= size
     assert stride == members
@@ -262,39 +292,55 @@
     up = [(i, i + 1) for i in range(members - 1)]
     down = [(i + 1, i) for i in range(members - 1)]
 
+    meta = jnp.concatenate([tile_rows, tile_cols, tile_count])
+
     def halo(head, tail):
         return lax.ppermute(tail, AXES, up), lax.ppermute(head, AXES, down)
 
     def sds(*shape):
         return jax.ShapeDtypeStruct(shape, F32)
 
-    left, right = halo(current_block[:, :width], current_block[:, rows_here - width :])
-    pleft, pright = halo(previous_block[:, :width], previous_block[:, rows_here - width :])
+    cut = rows_here - width
+    left, right = halo(
+        jnp.concatenate([current_block[:, :width], previous_block[:, :width]], axis=0),
+        jnp.concatenate([current_block[:, cut:], previous_block[:, cut:]], axis=0),
+    )
+    parts = pl.pallas_call(
+        split_kernel,
+        out_shape=jax.ShapeDtypeStruct((3, slots, tile, tile), BF16),
+        in_specs=[VMEM],
+        out_specs=VMEM,
+        compiler_params=pltpu.CompilerParams(vmem_limit_bytes=VMEM_LIMIT),
+        cost_estimate=pl.CostEstimate(flops=10**8, bytes_accessed=10**7, transcendentals=0),
+        name="split_tiles",
+    )(adjacency_tiles)
     x_image, head, tail = pl.pallas_call(
         functools.partial(first_kernel, tile),
         out_shape=(sds(k, rows_here), sds(k, width), sds(k, width)),
-        in_specs=[SMEM] * 3 + [VMEM] * 4,
+        in_specs=[SMEM] + [VMEM] * 4,
         out_specs=(VMEM,) * 3,
         scratch_shapes=[
             pltpu.VMEM((span, 3 * k, tile), BF16),
             pltpu.VMEM((row_tiles, k, tile), F32),
         ],
+        compiler_params=pltpu.CompilerParams(vmem_limit_bytes=VMEM_LIMIT),
         name="first_apply",
-    )(tile_rows, tile_cols, tile_count, current_block, left, right, adjacency_tiles)
+    )(meta, current_block, left, right, parts)
     aleft, aright = halo(head, tail)
     twice, message = pl.pallas_call(
         functools.partial(second_kernel, tile),
         out_shape=(sds(k, rows_here), sds(3 * k, LANES)),
-        in_specs=[SMEM] * 3 + [VMEM] * 8,
+        in_specs=[SMEM] + [VMEM] * 8,
         out_specs=(VMEM,) * 2,
         scratch_shapes=[
             pltpu.VMEM((span, 6 * k, tile), BF16),
             pltpu.VMEM((row_tiles, 2 * k, tile), F32),
             pltpu.VMEM((6 * k, rows_here), F32),
         ],
+        compiler_params=pltpu.CompilerParams(vmem_limit_bytes=VMEM_LIMIT),
         name="second_apply",
-    )(tile_rows, tile_cols, tile_count, current_block, previous_block, pleft, pright,
-      x_image, aleft, aright, adjacency_tiles)
+    )(meta, current_block, previous_block, left, right,
+      x_image, aleft, aright, parts)
     plan = stages(members)
     for number, (stride, size) in enumerate(plan):
         messages = [message] + [
@@ -307,13 +353,15 @@
                 out_shape=sds(3 * k, LANES),
                 in_specs=[VMEM] * size,
                 out_specs=VMEM,
-                name="merge",
+                compiler_params=pltpu.CompilerParams(vmem_limit_bytes=VMEM_LIMIT),
+        name="merge",
             )(*messages)
     return pl.pallas_call(
         functools.partial(last_kernel, len(messages), 1.0 / vertex_total),
         out_shape=(sds(k, rows_here), sds(k, rows_here), sds(3 * k, 3 * k)),
         in_specs=[SMEM] + [VMEM] * (len(messages) + 3),
         out_specs=(VMEM,) * 3,
+        compiler_params=pltpu.CompilerParams(vmem_limit_bytes=VMEM_LIMIT),
         name="finish",
     )(locked, *messages, current_block, x_image, twice)
 

time: 63.6 us -> 48 us (0.75)
  Pallas kernels: 21.3 us -> 12.3 us
  starting transfers between devices: 26.1 us -> 21.2 us
  local copies, waits for them, and re-layouts: 5.44 us -> 2.89 us
  waiting for transfers between devices: 8.21 us -> 9.15 us
    ppermute x6 -> x4, starting transfers between devices: 15.7 us -> 10.1 us  [halo(): return (lax.ppermute(tail, AXES, up), lax.ppermute(head, AXES, down))]
    pallas_call x1, Pallas kernels: 8.71 us -> 4.57 us  [body(): pl.pallas_call(functools.partial(last_kernel, len(messages), 1.0 / vertex...]
    pallas_call x1, Pallas kernels: 6.16 us -> 3.88 us  [body(): pl.pallas_call(functools.partial(second_kernel, tile), out_shape=(sds(k,...]
    pallas_call x1, Pallas kernels: 4.84 us -> 2.62 us  [body(): pl.pallas_call(functools.partial(first_kernel, tile), out_shape=(sds(k, r...]
    unnamed x24 -> x10, local copies, waits for them, and re-layouts: 3.67 us -> 1.9 us
    pallas_call x1 -> x3, Pallas kernels: 1.59 us -> 0.53 us  [body(): pl.pallas_call(merge_kernel, out_shape=sds(3 * k, LANES), in_specs=[VMEM]...]
    slice x1 -> x0, local copies, waits for them, and re-layouts: 0.88 us -> none  [body(): previous_block[:, :width]]
    ppermute x6 -> x4, starting transfers between devices: 10.5 us -> 11.1 us  [body(): lax.ppermute(message, AXES, [(i, i ^ m * stride) for i in range(members)])]
  transfers between devices with their start and end apart: 12 -> 8, of which waited for: 6 -> 5; matrix products, arithmetic and copies ran while one was open for 1% -> 0% of each run, Pallas kernels for 8% -> 1%
where the time goes in v2:
time: 48 us; the launch traced here: 47.8 us
  starting transfers between devices  21.2 us (44%)
  Pallas kernels  12.3 us (26%)
  waiting for transfers between devices  9.15 us (19%)
  local copies, waits for them, and re-layouts  2.89 us (6%)
  between operations  2.09 us (4%)
    ppermute x4, starting transfers between devices, body(): lax.ppermute(message, AXES, [(i, i ^ m * stride) for i in range(members)])  11.1 us
    ppermute x4, starting transfers between devices, halo(): return (lax.ppermute(tail, AXES, up), lax.ppermute(head, AXES, down))  10.1 us
    ppermute x4, waiting for transfers between devices, body(): lax.ppermute(message, AXES, [(i, i ^ m * stride) for i in range(members)])  6.39 us
    pallas_call x1, Pallas kernels, body(): pl.pallas_call(functools.partial(last_kernel, len(messages), 1.0 / vertex...  4.57 us
    pallas_call x1, Pallas kernels, body(): pl.pallas_call(functools.partial(second_kernel, tile), out_shape=(sds(k,...  3.88 us
    ppermute x4, waiting for transfers between devices, halo(): return (lax.ppermute(tail, AXES, up), lax.ppermute(head, AXES, down))  2.77 us
    pallas_call x1, Pallas kernels, body(): pl.pallas_call(functools.partial(first_kernel, tile), out_shape=(sds(k, r...  2.62 us
    unnamed x10, local copies, waits for them, and re-layouts  1.9 us
  transfers between devices with their start and end apart: 8, of which 5 were waited for; matrix products, arithmetic and copies ran while one was open for 0% of the time, Pallas kernels for 1%

profile of v2, /device:TPU:0, one launch (start us, length us, event | category | flops | bytes accessed | tf_op | source)
XLA Modules:
  0.0 47.8 jit_solution(614959389362259156)
XLA Ops:
  0.7 1.0 %fusion = (f32[16,1024]{1,0:T(8,128)S(1)}, f32[16,1024]{1,0:T(8,128)S(1)}, f32[16,1024]{1,0:T(8,128)S(1)}, f32[16,1024]{1,0:T(8,128)S(1)}) fusion(f32[16,2048]{1,0:T(8,128)} %refs_2_.1, f32[16,2048]{1,0:T(8,128)} %p_ref.1), kind=kLoop, calls=%fused_computation.3 | loop fusion | bytes 524288 | tf_op jit(solution)/shard_map/slice | solution.py:305
  1.7 1.3 %collective-permute-start.1 = (f32[32,1024]{1,0:T(8,128)S(1)}, f32[32,1024]{1,0:T(8,128)S(1)}, u32[]{:S(2)}, u32[]{:S(2)}) collective-permute-start(f32[32,1024]{1,0:T(8,128)S(1)} %pad_maximum_fusion.1), channel_id=1, source_target_pairs={{1,0},{2,1},{3,2},{4,3},{5,4},{6,5},{7,6},{8,7},{9,8},{10,9},{11,1... | collective-permute-start | bytes 393224 | tf_op jit(solution)/shard_map/ppermute | solution.py:298
  3.0 3.0 %collective-permute-start = (f32[32,1024]{1,0:T(8,128)S(1)}, f32[32,1024]{1,0:T(8,128)S(1)}, u32[]{:S(2)}, u32[]{:S(2)}) collective-permute-start(f32[32,1024]{1,0:T(8,128)S(1)} %pad_maximum_fusion), channel_id=1, source_target_pairs={{0,1},{1,2},{2,3},{3,4},{4,5},{5,6},{6,7},{7,8},{8,9},{9,10},{10,1... | collective-permute-start | bytes 393224 | tf_op jit(solution)/shard_map/ppermute | solution.py:298
  6.7 0.0 copy-start
  6.7 1.9 %copy-done = f32[48,128,128]{2,1,0:T(8,128)S(1)} copy-done((f32[48,128,128]{2,1,0:T(8,128)S(1)}, f32[48,128,128]{2,1,0:T(8,128)}, u32[]{:S(2)}) %copy-start) | copy-done | bytes 3145752
  8.6 0.7 %split_tiles.1.tiles_ref = bf16[3,48,128,128]{3,2,1,0:T(8,128)(2,1)S(1)} custom-call(f32[48,128,128]{2,1,0:T(8,128)S(1)} %copy-done), custom_call_target="tpu_custom_call" | custom-call | flops 100000000 | bytes 10000000 | tf_op jit(solution)/shard_map/split_tiles/pallas_call | solution.py:308
  9.3 0.1 pad_add_fusion.meta_ref
  9.4 2.6 %first_apply.1 = (f32[16,2048]{1,0:T(8,128)S(1)}, f32[16,1024]{1,0:T(8,128)S(1)}, f32[16,1024]{1,0:T(8,128)S(1)}) custom-call(s32[97]{0:T(128)S(1)} %pad_add_fusion.meta_ref, f32[16,2048]{1,0:T(8,128)S(1)} %copy-done.1, f32[32,1024]{1,0:T(8,128)S(1)} %collective-permute-done.left_ref.pleft_ref, f32[32,1024]{1,0:T(8,128)S(1)} %collective-permute-done.1.right_ref.pright_ref, ...), custom_call_target="tpu_custom_call" | custom-call | tf_op jit(solution)/shard_map/first_apply/pallas_call | solution.py:317
  12.0 4.5 %collective-permute-start.2 = (f32[16,1024]{1,0:T(8,128)S(1)}, f32[16,1024]{1,0:T(8,128)S(1)}, u32[]{:S(2)}, u32[]{:S(2)}) collective-permute-start(f32[16,1024]{1,0:T(8,128)S(1)} %get-tuple-element.9), channel_id=1, source_target_pairs={{0,1},{1,2},{2,3},{3,4},{4,5},{5,6},{6,7},{7,8},{8,9},{9,10},{10,1... | collective-permute-start | bytes 196616 | tf_op jit(solution)/shard_map/ppermute | solution.py:298
  16.5 1.3 %collective-permute-start.3 = (f32[16,1024]{1,0:T(8,128)S(1)}, f32[16,1024]{1,0:T(8,128)S(1)}, u32[]{:S(2)}, u32[]{:S(2)}) collective-permute-start(f32[16,1024]{1,0:T(8,128)S(1)} %get-tuple-element.10), channel_id=1, source_target_pairs={{1,0},{2,1},{3,2},{4,3},{5,4},{6,5},{7,6},{8,7},{9,8},{10,9},{11,1... | collective-permute-start | bytes 196616 | tf_op jit(solution)/shard_map/ppermute | solution.py:298
  17.8 2.8 %collective-permute-done.3.aright_ref = f32[16,1024]{1,0:T(8,128)S(1)} collective-permute-done((f32[16,1024]{1,0:T(8,128)S(1)}, f32[16,1024]{1,0:T(8,128)S(1)}, u32[]{:S(2)}, u32[]{:S(2)}) %collective-permute-start.3) | collective-permute-done | bytes 65568 | tf_op jit(solution)/shard_map/ppermute | solution.py:298
  20.6 3.9 %second_apply.1 = (f32[16,2048]{1,0:T(8,128)S(1)}, f32[48,128]{1,0:T(8,128)S(1)}) custom-call(s32[97]{0:T(128)S(1)} %pad_add_fusion.meta_ref, f32[16,2048]{1,0:T(8,128)S(1)} %copy-done.1, f32[16,2048]{1,0:T(8,128)S(1)} %copy-done.2, f32[32,1024]{1,0:T(8,128)S(1)} %collective-permute-done.left_ref.pleft_ref, ...), custom_call_target="tpu_custom_call" | custom-call | tf_op jit(solution)/shard_map/second_apply/pallas_call | solution.py:330
  24.5 3.0 %collective-permute-start.4 = (f32[48,128]{1,0:T(8,128)S(1)}, f32[48,128]{1,0:T(8,128)S(1)}, u32[]{:S(2)}, u32[]{:S(2)}) collective-permute-start(f32[48,128]{1,0:T(8,128)S(1)} %get-tuple-element.11.refs_0_), channel_id=1, source_target_pairs={{0,1},{1,0},{2,3},{3,2},{4,5},{5,4},{6,7},{7,6},{8,9},{9,8},{10,11... | collective-permute-start | bytes 73736 | tf_op jit(solution)/shard_map/ppermute | solution.py:347
  27.5 0.8 %collective-permute-done.4.refs_1_ = f32[48,128]{1,0:T(8,128)S(1)} collective-permute-done((f32[48,128]{1,0:T(8,128)S(1)}, f32[48,128]{1,0:T(8,128)S(1)}, u32[]{:S(2)}, u32[]{:S(2)}) %collective-permute-start.4) | collective-permute-done | bytes 24608 | tf_op jit(solution)/shard_map/ppermute | solution.py:347
  28.3 0.2 merge.3.refs_0_
  28.5 3.8 %collective-permute-start.5 = (f32[48,128]{1,0:T(8,128)S(1)}, f32[48,128]{1,0:T(8,128)S(1)}, u32[]{:S(2)}, u32[]{:S(2)}) collective-permute-start(f32[48,128]{1,0:T(8,128)S(1)} %merge.3.refs_0_), channel_id=1, source_target_pairs={{0,2},{1,3},{2,0},{3,1},{4,6},{5,7},{6,4},{7,5},{8,10},{9,11},{10,... | collective-permute-start | bytes 73736 | tf_op jit(solution)/shard_map/ppermute | solution.py:347
  32.3 1.8 %collective-permute-done.5.refs_1_ = f32[48,128]{1,0:T(8,128)S(1)} collective-permute-done((f32[48,128]{1,0:T(8,128)S(1)}, f32[48,128]{1,0:T(8,128)S(1)}, u32[]{:S(2)}, u32[]{:S(2)}) %collective-permute-start.5) | collective-permute-done | bytes 24608 | tf_op jit(solution)/shard_map/ppermute | solution.py:347
  34.1 0.2 merge.4.refs_0_
  34.3 1.6 %collective-permute-start.6 = (f32[48,128]{1,0:T(8,128)S(1)}, f32[48,128]{1,0:T(8,128)S(1)}, u32[]{:S(2)}, u32[]{:S(2)}) collective-permute-start(f32[48,128]{1,0:T(8,128)S(1)} %merge.4.refs_0_), channel_id=1, source_target_pairs={{0,4},{1,5},{2,6},{3,7},{4,0},{5,1},{6,2},{7,3},{8,12},{9,13},{10,... | collective-permute-start | bytes 73736 | tf_op jit(solution)/shard_map/ppermute | solution.py:347
  36.0 2.2 %collective-permute-done.6.refs_1_ = f32[48,128]{1,0:T(8,128)S(1)} collective-permute-done((f32[48,128]{1,0:T(8,128)S(1)}, f32[48,128]{1,0:T(8,128)S(1)}, u32[]{:S(2)}, u32[]{:S(2)}) %collective-permute-start.6) | collective-permute-done | bytes 24608 | tf_op jit(solution)/shard_map/ppermute | solution.py:347
  38.2 0.2 merge.5.refs_0_
  38.4 2.7 %collective-permute-start.7 = (f32[48,128]{1,0:T(8,128)S(1)}, f32[48,128]{1,0:T(8,128)S(1)}, u32[]{:S(2)}, u32[]{:S(2)}) collective-permute-start(f32[48,128]{1,0:T(8,128)S(1)} %merge.5.refs_0_), channel_id=1, source_target_pairs={{0,8},{1,9},{2,10},{3,11},{4,12},{5,13},{6,14},{7,15},{8,0},{9,1},... | collective-permute-start | bytes 73736 | tf_op jit(solution)/shard_map/ppermute | solution.py:347
  41.7 1.5 %collective-permute-done.7.refs_1_ = f32[48,128]{1,0:T(8,128)S(1)} collective-permute-done((f32[48,128]{1,0:T(8,128)S(1)}, f32[48,128]{1,0:T(8,128)S(1)}, u32[]{:S(2)}, u32[]{:S(2)}) %collective-permute-start.7) | collective-permute-done | bytes 24608 | tf_op jit(solution)/shard_map/ppermute | solution.py:347
  43.2 4.6 %finish.1 = (f32[16,2048]{1,0:T(8,128)}, f32[16,2048]{1,0:T(8,128)}, f32[48,48]{1,0:T(8,128)}) custom-call(s32[1]{0:T(128)S(6)} %copy.11.locked_ref, f32[48,128]{1,0:T(8,128)S(1)} %merge.5.refs_0_, f32[48,128]{1,0:T(8,128)S(1)} %collective-permute-done.7.refs_1_, f32[16,2048]{1,0:T(8,128)S(1)} %copy-done.1, f32[16,2048]{1,0:T(8,128)S(1)} %get-tuple-element.8.ax_ref.refs_3_, ...), custom_call_target="tpu_custom_call" | custom-call | tf_op jit(solution)/shard_map/finish/pallas_call | solution.py:359
  (13 shorter events, 0.0 us)
Async XLA Ops:
  0.6 8.7 %copy-start.1 = (f32[16,2048]{1,0:T(8,128)S(1)}, f32[16,2048]{1,0:T(8,128)}, u32[]{:S(2)}) copy-start(f32[16,2048]{1,0:T(8,128)} %refs_2_.1) | copy-start | bytes 393220
  0.6 8.6 %copy-start.4 = (s32[48]{0:T(128)S(1)}, s32[48]{0:T(128)}, u32[]{:S(2)}) copy-start(s32[48]{0:T(128)} %param.10) | copy-start | bytes 580
  0.7 8.6 %copy-start.3 = (s32[48]{0:T(128)S(1)}, s32[48]{0:T(128)}, u32[]{:S(2)}) copy-start(s32[48]{0:T(128)} %param.11) | copy-start | bytes 580
  1.7 7.7 %collective-permute-start.1 = (f32[32,1024]{1,0:T(8,128)S(1)}, f32[32,1024]{1,0:T(8,128)S(1)}, u32[]{:S(2)}, u32[]{:S(2)}) collective-permute-start(f32[32,1024]{1,0:T(8,128)S(1)} %pad_maximum_fusion.1), channel_id=1, source_target_pairs={{1,0},{2,1},{3,2},{4,3},{5,4},{6,5},{7,6},{8,7},{9,8},{10,9},{11,1... | collective-permute-start | bytes 393224 | tf_op jit(solution)/shard_map/ppermute | solution.py:298
  3.0 6.4 %collective-permute-start = (f32[32,1024]{1,0:T(8,128)S(1)}, f32[32,1024]{1,0:T(8,128)S(1)}, u32[]{:S(2)}, u32[]{:S(2)}) collective-permute-start(f32[32,1024]{1,0:T(8,128)S(1)} %pad_maximum_fusion), channel_id=1, source_target_pairs={{0,1},{1,2},{2,3},{3,4},{4,5},{5,6},{6,7},{7,8},{8,9},{9,10},{10,1... | collective-permute-start | bytes 393224 | tf_op jit(solution)/shard_map/ppermute | solution.py:298
  6.7 1.9 %copy-start = (f32[48,128,128]{2,1,0:T(8,128)S(1)}, f32[48,128,128]{2,1,0:T(8,128)}, u32[]{:S(2)}) copy-start(f32[48,128,128]{2,1,0:T(8,128)} %tiles_ref.1) | copy-start | bytes 9437188
  8.6 12.0 %copy-start.2 = (f32[16,2048]{1,0:T(8,128)S(1)}, f32[16,2048]{1,0:T(8,128)}, u32[]{:S(2)}) copy-start(f32[16,2048]{1,0:T(8,128)} %p_ref.1) | copy-start | bytes 393220
  12.0 5.8 %collective-permute-start.2 = (f32[16,1024]{1,0:T(8,128)S(1)}, f32[16,1024]{1,0:T(8,128)S(1)}, u32[]{:S(2)}, u32[]{:S(2)}) collective-permute-start(f32[16,1024]{1,0:T(8,128)S(1)} %get-tuple-element.9), channel_id=1, source_target_pairs={{0,1},{1,2},{2,3},{3,4},{4,5},{5,6},{6,7},{7,8},{8,9},{9,10},{10,1... | collective-permute-start | bytes 196616 | tf_op jit(solution)/shard_map/ppermute | solution.py:298
  16.5 4.1 %collective-permute-start.3 = (f32[16,1024]{1,0:T(8,128)S(1)}, f32[16,1024]{1,0:T(8,128)S(1)}, u32[]{:S(2)}, u32[]{:S(2)}) collective-permute-start(f32[16,1024]{1,0:T(8,128)S(1)} %get-tuple-element.10), channel_id=1, source_target_pairs={{1,0},{2,1},{3,2},{4,3},{5,4},{6,5},{7,6},{8,7},{9,8},{10,9},{11,1... | collective-permute-start | bytes 196616 | tf_op jit(solution)/shard_map/ppermute | solution.py:298
  24.5 3.8 %collective-permute-start.4 = (f32[48,128]{1,0:T(8,128)S(1)}, f32[48,128]{1,0:T(8,128)S(1)}, u32[]{:S(2)}, u32[]{:S(2)}) collective-permute-start(f32[48,128]{1,0:T(8,128)S(1)} %get-tuple-element.11.refs_0_), channel_id=1, source_target_pairs={{0,1},{1,0},{2,3},{3,2},{4,5},{5,4},{6,7},{7,6},{8,9},{9,8},{10,11... | collective-permute-start | bytes 73736 | tf_op jit(solution)/shard_map/ppermute | solution.py:347
  28.5 5.6 %collective-permute-start.5 = (f32[48,128]{1,0:T(8,128)S(1)}, f32[48,128]{1,0:T(8,128)S(1)}, u32[]{:S(2)}, u32[]{:S(2)}) collective-permute-start(f32[48,128]{1,0:T(8,128)S(1)} %merge.3.refs_0_), channel_id=1, source_target_pairs={{0,2},{1,3},{2,0},{3,1},{4,6},{5,7},{6,4},{7,5},{8,10},{9,11},{10,... | collective-permute-start | bytes 73736 | tf_op jit(solution)/shard_map/ppermute | solution.py:347
  34.3 3.9 %collective-permute-start.6 = (f32[48,128]{1,0:T(8,128)S(1)}, f32[48,128]{1,0:T(8,128)S(1)}, u32[]{:S(2)}, u32[]{:S(2)}) collective-permute-start(f32[48,128]{1,0:T(8,128)S(1)} %merge.4.refs_0_), channel_id=1, source_target_pairs={{0,4},{1,5},{2,6},{3,7},{4,0},{5,1},{6,2},{7,3},{8,12},{9,13},{10,... | collective-permute-start | bytes 73736 | tf_op jit(solution)/shard_map/ppermute | solution.py:347
  38.4 4.8 %collective-permute-start.7 = (f32[48,128]{1,0:T(8,128)S(1)}, f32[48,128]{1,0:T(8,128)S(1)}, u32[]{:S(2)}, u32[]{:S(2)}) collective-permute-start(f32[48,128]{1,0:T(8,128)S(1)} %merge.5.refs_0_), channel_id=1, source_target_pairs={{0,8},{1,9},{2,10},{3,11},{4,12},{5,13},{6,14},{7,15},{8,0},{9,1},... | collective-permute-start | bytes 73736 | tf_op jit(solution)/shard_map/ppermute | solution.py:347

commit v3 on v2

--- a/solution.py
+++ b/solution.py
@@ -13,7 +13,7 @@
 HIGHEST = lax.Precision.HIGHEST
 LANES = 128
 UNROLL = 8
-GROUP = 4
+GROUP = 8
 VMEM_LIMIT = 24 * 1024 * 1024
 VMEM = pl.BlockSpec(memory_space=pltpu.VMEM)
 SMEM = pl.BlockSpec(memory_space=pltpu.SMEM)
@@ -33,15 +33,19 @@
         parts_ref[tile, k * height + at : k * height + at + channels, :] = part
 
 
-def load_span(parts_ref, at, height, left_ref, mid_ref, right_ref, tile):
-    reach = left_ref.shape[1] // tile
-    rows = mid_ref.shape[1] // tile
+def load_edges(parts_ref, at, height, first_ref, second_ref, rows, tile, odd):
+    reach = first_ref.shape[1] // tile
+    first = jnp.where(odd, 0, reach + rows)
+    second = reach + rows - first
     for k in range(reach):
         cut = slice(k * tile, (k + 1) * tile)
-        store_parts(parts_ref, k, at, height, left_ref[:, cut])
-        store_parts(parts_ref, reach + rows + k, at, height, right_ref[:, cut])
-    for k in range(rows):
-        store_parts(parts_ref, reach + k, at, height, mid_ref[:, k * tile : (k + 1) * tile])
+        store_parts(parts_ref, first + k, at, height, first_ref[:, cut])
+        store_parts(parts_ref, second + k, at, height, second_ref[:, cut])
+
+
+def load_middle(parts_ref, offset, at, height, mid_ref, tile):
+    for k in range(mid_ref.shape[1] // tile):
+        store_parts(parts_ref, offset + k, at, height, mid_ref[:, k * tile : (k + 1) * tile])
 
 
 def tile_product(parts_ref, tiles_ref, t, col, height):
@@ -54,59 +58,80 @@
     return y1[:h] + ((y1[h : 2 * h] + y2[:h]) + (y1[2 * h :] + y2[h : 2 * h] + y3))
 
 
-def apply_tiles(parts_ref, sums_ref, tiles_ref, meta_ref, height, reach):
+def diagonal_tiles(parts_ref, sums_ref, tiles_ref, height, start, stop):
+    def step(index, carry):
+        for u in range(UNROLL):
+            t = index * UNROLL + u
+            sums_ref[t] = tile_product(parts_ref, tiles_ref, t, t, height)
+        return carry
+
+    lax.fori_loop(start // UNROLL, stop // UNROLL, step, 0)
+
+
+def extra_tiles(parts_ref, sums_ref, tiles_ref, meta_ref, height, reach):
     row_tiles = sums_ref.shape[0]
     slots = tiles_ref.shape[1]
     base = meta_ref[0]
     count = meta_ref[2 * slots]
 
-    def diagonal(step, carry):
-        for u in range(UNROLL):
-            t = step * UNROLL + u
-            sums_ref[t] = tile_product(parts_ref, tiles_ref, t, t + reach, height)
-        return carry
-
-    lax.fori_loop(0, row_tiles // UNROLL, diagonal, 0)
-
-    def extra(step, carry):
+    def step(index, carry):
         found = []
         for u in range(UNROLL):
-            t = row_tiles + step * UNROLL + u
+            t = row_tiles + index * UNROLL + u
             y = tile_product(parts_ref, tiles_ref, t, meta_ref[slots + t] - base + reach, height)
             found.append((meta_ref[t] - base, jnp.where(t < count, y, 0.0)))
         for row, y in found:
             sums_ref[row] += y
         return carry
 
-    lax.fori_loop(0, (slots - row_tiles) // UNROLL, extra, 0)
-
-
-def split_kernel(tiles_ref, out_ref):
-    def step(t, carry):
-        for u in range(2):
-            for k, part in enumerate(split3(tiles_ref[2 * t + u])):
-                out_ref[k, 2 * t + u] = part
-        return carry
-
-    lax.fori_loop(0, tiles_ref.shape[0] // 2, step, 0)
-
-
-def first_kernel(tile, meta_ref, x_ref, left_ref, right_ref, tiles_ref,
-                 image_ref, head_ref, tail_ref, parts_ref, sums_ref):
+    lax.fori_loop(0, (slots - row_tiles) // UNROLL, step, 0)
+
+
+def split_kernel(tiles_hbm, x_ref, out_ref, sums_ref, tiles_ref, parts_ref, sems):
+    row_tiles, k_rows, tile = sums_ref.shape
+    slots = tiles_ref.shape[0]
+    chunks = sems.shape[0]
+    size = slots // chunks
+
+    def copy(c):
+        part = pl.ds(c * size, size)
+        return pltpu.make_async_copy(tiles_hbm.at[part], tiles_ref.at[part], sems.at[c])
+
+    for c in range(chunks):
+        copy(c).start()
+    load_middle(parts_ref, 0, 0, k_rows, x_ref, tile)
+    for c in range(chunks):
+        copy(c).wait()
+
+        def step(t, carry):
+            for k, part in enumerate(split3(tiles_ref[t])):
+                out_ref[k, t] = part
+            return carry
+
+        lax.fori_loop(c * size, (c + 1) * size, step, 0, unroll=2)
+        if (c + 1) * size <= row_tiles:
+            diagonal_tiles(parts_ref, sums_ref, out_ref, k_rows, c * size, (c + 1) * size)
+
+
+def first_kernel(tile, meta_ref, x_ref, left_ref, right_ref, tiles_ref, start_ref,
+                 image_ref, first_ref, second_ref, parts_ref, sums_ref):
     channels = x_ref.shape[0]
     reach = left_ref.shape[1] // tile
     row_tiles = sums_ref.shape[0]
-    load_span(parts_ref, 0, channels, left_ref.at[0:channels], x_ref, right_ref.at[0:channels], tile)
-    apply_tiles(parts_ref, sums_ref, tiles_ref, meta_ref, channels, reach)
+    odd = meta_ref[2 * tiles_ref.shape[1] + 1] == 1
+    load_middle(parts_ref, reach, 0, channels, x_ref, tile)
+    load_edges(parts_ref, 0, channels, left_ref.at[0:channels], right_ref.at[0:channels],
+               row_tiles, tile, odd)
+    sums_ref[...] = start_ref[...]
+    extra_tiles(parts_ref, sums_ref, tiles_ref, meta_ref, channels, reach)
     for i in range(row_tiles):
         cut = slice(i * tile, (i + 1) * tile)
-        value = x_ref[:, cut] - sums_ref[i]
-        image_ref[:, cut] = value
-        if i < reach:
-            head_ref[:, cut] = value
-        if i >= row_tiles - reach:
-            k = i - (row_tiles - reach)
-            tail_ref[:, k * tile : (k + 1) * tile] = value
+        image_ref[:, cut] = x_ref[:, cut] - sums_ref[i]
+    far = (row_tiles - reach) * tile
+    head = image_ref[:, : reach * tile]
+    tail = image_ref[:, far:]
+    first_ref[...] = jnp.where(odd, head, tail)
+    second_ref[...] = jnp.where(odd, tail, head)
 
 
 def iota2(shape, dim):
@@ -118,15 +143,12 @@
                            preferred_element_type=F32)
 
 
-def second_kernel(tile, meta_ref, x_ref, p_ref, pleft_ref, pright_ref,
-                  ax_ref, aleft_ref, aright_ref, tiles_ref, a2x_ref, message_ref,
-                  parts_ref, sums_ref, basis_ref):
+def middle_kernel(tile, x_ref, p_ref, ax_ref, tiles_ref,
+                  sums_ref, basis_ref, quotient_ref, message_ref, parts_ref):
     k = x_ref.shape[0]
-    reach = aleft_ref.shape[1] // tile
-    row_tiles = sums_ref.shape[0]
-    load_span(parts_ref, k, 2 * k, pleft_ref.at[k : 2 * k], p_ref, pright_ref.at[k : 2 * k], tile)
-    load_span(parts_ref, 0, 2 * k, aleft_ref, ax_ref, aright_ref, tile)
-    apply_tiles(parts_ref, sums_ref, tiles_ref, meta_ref, 2 * k, reach)
+    load_middle(parts_ref, 0, 0, 2 * k, ax_ref, tile)
+    load_middle(parts_ref, 0, k, 2 * k, p_ref, tile)
+    diagonal_tiles(parts_ref, sums_ref, tiles_ref, 2 * k, 0, sums_ref.shape[0])
     x = x_ref[...]
     ax = ax_ref[...]
     q = jnp.sum(x * ax, axis=1, keepdims=True) / (jnp.sum(x * x, axis=1, keepdims=True) + 1e-06)
@@ -134,18 +156,37 @@
     basis_ref[k : 2 * k, :] = ax - q * x
     basis_ref[2 * k : 3 * k, :] = p_ref[...]
     basis_ref[3 * k : 4 * k, :] = ax
+    quotient_ref[...] = jnp.broadcast_to(q, quotient_ref.shape)
+    message_ref[...] = jnp.zeros_like(message_ref)
+    message_ref[:, 0 : 4 * k] = dot_nt(basis_ref[0 : 3 * k, :], basis_ref[...])
+    place = iota2((k, LANES), 1) == iota2((k, LANES), 0) + 6 * k
+    message_ref[0:k, :] = jnp.where(place, q, message_ref[0:k, :])
+
+
+def second_kernel(tile, meta_ref, p_ref, pleft_ref, pright_ref, ax_ref, aleft_ref, aright_ref,
+                  tiles_ref, start_ref, basis_ref, quotient_ref, begun_ref,
+                  a2x_ref, message_ref, parts_ref, sums_ref, images_ref):
+    k = p_ref.shape[0]
+    reach = aleft_ref.shape[1] // tile
+    row_tiles = sums_ref.shape[0]
+    odd = meta_ref[2 * tiles_ref.shape[1] + 1] == 1
+    load_middle(parts_ref, reach, 0, 2 * k, ax_ref, tile)
+    load_middle(parts_ref, reach, k, 2 * k, p_ref, tile)
+    load_edges(parts_ref, k, 2 * k, pleft_ref.at[k : 2 * k], pright_ref.at[k : 2 * k],
+               row_tiles, tile, odd)
+    load_edges(parts_ref, 0, 2 * k, aleft_ref, aright_ref, row_tiles, tile, odd)
+    sums_ref[...] = start_ref[...]
+    extra_tiles(parts_ref, sums_ref, tiles_ref, meta_ref, 2 * k, reach)
+    q = quotient_ref[:, 0:1]
     for i in range(row_tiles):
         cut = slice(i * tile, (i + 1) * tile)
         total = sums_ref[i]
         twice = ax_ref[:, cut] - total[:k]
         a2x_ref[:, cut] = twice
-        basis_ref[4 * k : 5 * k, cut] = twice - q * ax_ref[:, cut]
-        basis_ref[5 * k : 6 * k, cut] = p_ref[:, cut] - total[k:]
-    grams = dot_nt(basis_ref[0 : 3 * k, :], basis_ref[...])
-    message_ref[...] = jnp.zeros_like(message_ref)
-    message_ref[:, 0 : 6 * k] = grams
-    place = iota2((k, LANES), 1) == iota2((k, LANES), 0) + 6 * k
-    message_ref[0:k, :] = jnp.where(place, q, message_ref[0:k, :])
+        images_ref[0:k, cut] = twice - q * ax_ref[:, cut]
+        images_ref[k : 2 * k, cut] = p_ref[:, cut] - total[k:]
+    message_ref[...] = begun_ref[...]
+    message_ref[:, 4 * k : 6 * k] = dot_nt(basis_ref[0 : 3 * k, :], images_ref[...])
 
 
 def tree(values):
@@ -289,58 +330,81 @@
     reach = row_tiles // 2
     width = reach * tile
     span = row_tiles + 2 * reach
-    up = [(i, i + 1) for i in range(members - 1)]
-    down = [(i + 1, i) for i in range(members - 1)]
-
-    meta = jnp.concatenate([tile_rows, tile_cols, tile_count])
-
-    def halo(head, tail):
-        return lax.ppermute(tail, AXES, up), lax.ppermute(head, AXES, down)
+    inner = [(i, i ^ 1) for i in range(members)]
+    outer = [(i, i + 1 if i % 2 else i - 1) for i in range(1, members - 1)]
+    odd = lax.axis_index(AXES) % 2
+    meta = jnp.concatenate([tile_rows, tile_cols, tile_count, odd[None].astype(jnp.int32)])
+
+    def halo(first, second):
+        return lax.ppermute(first, AXES, inner), lax.ppermute(second, AXES, outer)
 
     def sds(*shape):
         return jax.ShapeDtypeStruct(shape, F32)
 
-    cut = rows_here - width
-    left, right = halo(
-        jnp.concatenate([current_block[:, :width], previous_block[:, :width]], axis=0),
-        jnp.concatenate([current_block[:, cut:], previous_block[:, cut:]], axis=0),
-    )
-    parts = pl.pallas_call(
+    def edge(start):
+        return jnp.concatenate(
+            [
+                lax.dynamic_slice_in_dim(block, start * (rows_here - width), width, 1)
+                for block in (current_block, previous_block)
+            ],
+            axis=0,
+        )
+
+    left, right = halo(edge(1 - odd), edge(odd))
+    params = pltpu.CompilerParams(vmem_limit_bytes=VMEM_LIMIT)
+    cost = pl.CostEstimate(flops=10**8, bytes_accessed=10**7, transcendentals=0)
+    parts, x_sums = pl.pallas_call(
         split_kernel,
-        out_shape=jax.ShapeDtypeStruct((3, slots, tile, tile), BF16),
-        in_specs=[VMEM],
-        out_specs=VMEM,
-        compiler_params=pltpu.CompilerParams(vmem_limit_bytes=VMEM_LIMIT),
-        cost_estimate=pl.CostEstimate(flops=10**8, bytes_accessed=10**7, transcendentals=0),
+        out_shape=(jax.ShapeDtypeStruct((3, slots, tile, tile), BF16), sds(row_tiles, k, tile)),
+        in_specs=[pl.BlockSpec(memory_space=pltpu.HBM), VMEM],
+        out_specs=(VMEM,) * 2,
+        scratch_shapes=[
+            pltpu.VMEM((slots, tile, tile), F32),
+            pltpu.VMEM((row_tiles, 3 * k, tile), BF16),
+            pltpu.SemaphoreType.DMA((slots // UNROLL,)),
+        ],
+        compiler_params=params,
+        cost_estimate=cost,
         name="split_tiles",
-    )(adjacency_tiles)
+    )(adjacency_tiles, current_block)
     x_image, head, tail = pl.pallas_call(
         functools.partial(first_kernel, tile),
         out_shape=(sds(k, rows_here), sds(k, width), sds(k, width)),
-        in_specs=[SMEM] + [VMEM] * 4,
+        in_specs=[SMEM] + [VMEM] * 5,
         out_specs=(VMEM,) * 3,
         scratch_shapes=[
             pltpu.VMEM((span, 3 * k, tile), BF16),
             pltpu.VMEM((row_tiles, k, tile), F32),
         ],
-        compiler_params=pltpu.CompilerParams(vmem_limit_bytes=VMEM_LIMIT),
+        compiler_params=params,
         name="first_apply",
-    )(meta, current_block, left, right, parts)
+    )(meta, current_block, left, right, parts, x_sums)
     aleft, aright = halo(head, tail)
+    sums, basis, quotient, begun = pl.pallas_call(
+        functools.partial(middle_kernel, tile),
+        out_shape=(sds(row_tiles, 2 * k, tile), sds(4 * k, rows_here), sds(k, LANES),
+                   sds(3 * k, LANES)),
+        in_specs=[VMEM] * 4,
+        out_specs=(VMEM,) * 4,
+        scratch_shapes=[pltpu.VMEM((row_tiles, 6 * k, tile), BF16)],
+        compiler_params=params,
+        cost_estimate=cost,
+        name="middle",
+    )(current_block, previous_block, x_image, parts)
     twice, message = pl.pallas_call(
         functools.partial(second_kernel, tile),
         out_shape=(sds(k, rows_here), sds(3 * k, LANES)),
-        in_specs=[SMEM] + [VMEM] * 8,
+        in_specs=[SMEM] + [VMEM] * 11,
         out_specs=(VMEM,) * 2,
         scratch_shapes=[
             pltpu.VMEM((span, 6 * k, tile), BF16),
             pltpu.VMEM((row_tiles, 2 * k, tile), F32),
-            pltpu.VMEM((6 * k, rows_here), F32),
+            pltpu.VMEM((2 * k, rows_here), F32),
         ],
-        compiler_params=pltpu.CompilerParams(vmem_limit_bytes=VMEM_LIMIT),
+        compiler_params=params,
         name="second_apply",
-    )(meta, current_block, previous_block, left, right,
-      x_image, aleft, aright, parts)
+    )(meta, previous_block, left, right, x_image, aleft, aright, parts, sums, basis, quotient,
+      begun)
     plan = stages(members)
     for number, (stride, size) in enumerate(plan):
         messages = [message] + [

time: 48 us -> 41.8 us (0.87)
  starting transfers between devices: 21.2 us -> 17.4 us
  waiting for transfers between devices: 9.15 us -> 5.63 us
  local copies, waits for them, and re-layouts: 2.89 us -> 3.79 us
  other arithmetic: 0.1 us -> 0.77 us
    ppermute x4, starting transfers between devices: 10.1 us -> 5.8 us  [halo(): return (lax.ppermute(first, AXES, inner), lax.ppermute(second, AXES, outer))]
    ppermute x4, waiting for transfers between devices: 2.77 us -> 0.01 us  [halo(): return (lax.ppermute(first, AXES, inner), lax.ppermute(second, AXES, outer))]
    pallas_call x1 -> x2, Pallas kernels: 0.66 us -> 3.05 us  [the longest x1 1.62 us: body(): pl.pallas_call(split_kernel, out_shape=(jax.ShapeDtypeStruct((3, slots, t...]
    pallas_call x1, Pallas kernels: 3.88 us -> 2.68 us  [body(): pl.pallas_call(functools.partial(second_kernel, tile), out_shape=(sds(k,...]
    dynamic_slice x0 -> x1, local copies, waits for them, and re-layouts: none -> 0.99 us  [edge(): lax.dynamic_slice_in_dim(block, start * (rows_here - width), width, 1)]
    slice x1 -> x0, local copies, waits for them, and re-layouts: 0.99 us -> none  [body(): current_block[:, :width]]
    pallas_call x1, Pallas kernels: 4.57 us -> 3.67 us  [body(): pl.pallas_call(functools.partial(last_kernel, len(messages), 1.0 / vertex...]
    unnamed x10 -> x6, local copies, waits for them, and re-layouts: 1.9 us -> 2.79 us
  transfers between devices with their start and end apart: 8 -> 8, of which waited for: 5 -> 4; matrix products, arithmetic and copies ran while one was open for 0% -> 2% of each run, Pallas kernels for 1% -> 7%
where the time goes in v3:
time: 41.8 us; the launch traced here: 41.6 us
  starting transfers between devices  17.4 us (42%)
  Pallas kernels  11.9 us (28%)
  waiting for transfers between devices  5.63 us (13%)
  local copies, waits for them, and re-layouts  3.79 us (9%)
  between operations  2.09 us (5%)
  other arithmetic  0.77 us (2%)
    ppermute x4, starting transfers between devices, body(): lax.ppermute(message, AXES, [(i, i ^ m * stride) for i in range(members)])  11.6 us
    ppermute x4, starting transfers between devices, halo(): return (lax.ppermute(first, AXES, inner), lax.ppermute(second, AXES, outer))  5.8 us
    ppermute x4, waiting for transfers between devices, body(): lax.ppermute(message, AXES, [(i, i ^ m * stride) for i in range(members)])  5.62 us
    pallas_call x1, Pallas kernels, body(): pl.pallas_call(functools.partial(last_kernel, len(messages), 1.0 / vertex...  3.67 us
    unnamed x6, local copies, waits for them, and re-layouts  2.79 us
    pallas_call x1, Pallas kernels, body(): pl.pallas_call(functools.partial(second_kernel, tile), out_shape=(sds(k,...  2.68 us
    pallas_call x1, Pallas kernels, body(): pl.pallas_call(functools.partial(first_kernel, tile), out_shape=(sds(k, r...  1.96 us
    pallas_call x1, Pallas kernels, body(): pl.pallas_call(split_kernel, out_shape=(jax.ShapeDtypeStruct((3, slots, t...  1.62 us
  transfers between devices with their start and end apart: 8, of which 4 were waited for; matrix products, arithmetic and copies ran while one was open for 2% of the time, Pallas kernels for 7%

profile of v3, /device:TPU:0, one launch (start us, length us, event | category | flops | bytes accessed | tf_op | source)
XLA Modules:
  0.0 41.6 jit_solution(18338126519505855547)
XLA Ops:
  0.7 1.0 %constant_dynamic-slice_fusion = (f32[16,1024]{1,0:T(8,128)S(1)}, f32[16,1024]{1,0:T(8,128)S(1)}, f32[16,1024]{1,0:T(8,128)S(1)}, f32[16,1024]{1,0:T(8,128)S(1)}) fusion(f32[16,2048]{1,0:T(8,128)} %p_ref.3, s32[]{:T(128)S(6)} %select_n.17, s32[]{:T(128)S(6)} %select_n.16, f32[16,2048]{1,0:T(8,128)} %refs_2_.1), kind=kLoop, calls=%fused_computation.2 | loop fusion | bytes 524296 | tf_op jit(solution)/shard_map/dynamic_slice | solution.py:347
  1.7 0.7 %collective-permute-start.1 = (f32[32,1024]{1,0:T(8,128)S(1)}, f32[32,1024]{1,0:T(8,128)S(1)}, u32[]{:S(2)}, u32[]{:S(2)}) collective-permute-start(f32[32,1024]{1,0:T(8,128)S(1)} %pad_maximum_fusion.1), channel_id=1, source_target_pairs={{1,2},{2,1},{3,4},{4,3},{5,6},{6,5},{7,8},{8,7},{9,10},{10,9},{11,... | collective-permute-start | bytes 393224 | tf_op jit(solution)/shard_map/ppermute | solution.py:339
  2.4 4.4 %collective-permute-start = (f32[32,1024]{1,0:T(8,128)S(1)}, f32[32,1024]{1,0:T(8,128)S(1)}, u32[]{:S(2)}, u32[]{:S(2)}) collective-permute-start(f32[32,1024]{1,0:T(8,128)S(1)} %pad_maximum_fusion), channel_id=1, source_target_pairs={{0,1},{1,0},{2,3},{3,2},{4,5},{5,4},{6,7},{7,6},{8,9},{9,8},{10,11... | collective-permute-start | bytes 393224 | tf_op jit(solution)/shard_map/ppermute | solution.py:339
  7.4 0.9 %copy-done = f32[16,2048]{1,0:T(8,128)S(1)} copy-done((f32[16,2048]{1,0:T(8,128)S(1)}, f32[16,2048]{1,0:T(8,128)}, u32[]{:S(2)}) %copy-start) | copy-done | bytes 131096
  8.3 1.9 %copy-done.1 = f32[48,128,128]{2,1,0:T(8,128)S(1)} copy-done((f32[48,128,128]{2,1,0:T(8,128)S(1)}, f32[48,128,128]{2,1,0:T(8,128)}, u32[]{:S(2)}) %copy-start.1) | copy-done | bytes 3145752
  10.2 1.6 %split_tiles.1 = (bf16[3,48,128,128]{3,2,1,0:T(8,128)(2,1)S(1)}, f32[16,16,128]{2,1,0:T(8,128)S(1)}) custom-call(f32[48,128,128]{2,1,0:T(8,128)S(1)} %copy-done.1, f32[16,2048]{1,0:T(8,128)S(1)} %copy-done), custom_call_target="tpu_custom_call" | custom-call | flops 100000000 | bytes 10000000 | tf_op jit(solution)/shard_map/split_tiles/pallas_call | solution.py:356
  11.8 0.8 %pad_add_fusion.meta_ref = s32[98]{0:T(128)S(1)} fusion(s32[1]{0:T(128)} %bitcast, s32[1]{0:T(128)S(6)} %copy.10, s32[48]{0:T(128)} %param.11, s32[48]{0:T(128)} %param.10), kind=kLoop, calls=%fused_computation.6 | loop fusion | flops 294 | bytes 784 | tf_op jit(solution)/shard_map/concatenate | solution.py:336
  12.6 2.0 %first_apply.1 = (f32[16,2048]{1,0:T(8,128)S(1)}, f32[16,1024]{1,0:T(8,128)S(1)}, f32[16,1024]{1,0:T(8,128)S(1)}) custom-call(s32[98]{0:T(128)S(1)} %pad_add_fusion.meta_ref, f32[16,2048]{1,0:T(8,128)S(1)} %copy-done, f32[32,1024]{1,0:T(8,128)S(1)} %collective-permute-done.left_ref.pleft_ref, f32[32,1024]{1,0:T(8,128)S(1)} %collective-permute-done.1.right_ref.pright_ref, ...), custom_call_target="tpu_custom_call" | custom-call | tf_op jit(solution)/shard_map/first_apply/pallas_call | solution.py:370
  14.6 0.1 collective-permute-start.2
  14.6 0.7 %collective-permute-start.3 = (f32[16,1024]{1,0:T(8,128)S(1)}, f32[16,1024]{1,0:T(8,128)S(1)}, u32[]{:S(2)}, u32[]{:S(2)}) collective-permute-start(f32[16,1024]{1,0:T(8,128)S(1)} %get-tuple-element.18), channel_id=1, source_target_pairs={{1,2},{2,1},{3,4},{4,3},{5,6},{6,5},{7,8},{8,7},{9,10},{10,9},{11,... | collective-permute-start | bytes 196616 | tf_op jit(solution)/shard_map/ppermute | solution.py:339
  15.3 1.4 %middle.1 = (f32[16,32,128]{2,1,0:T(8,128)S(1)}, f32[64,2048]{1,0:T(8,128)S(1)}, f32[16,128]{1,0:T(8,128)S(1)}, f32[48,128]{1,0:T(8,128)S(1)}) custom-call(f32[16,2048]{1,0:T(8,128)S(1)} %copy-done, f32[16,2048]{1,0:T(8,128)S(1)} %copy-done.2, f32[16,2048]{1,0:T(8,128)S(1)} %get-tuple-element.16.ax_ref.refs_3_, ...), custom_call_target="tpu_custom_call" | custom-call | flops 100000000 | bytes 10000000 | tf_op jit(solution)/shard_map/middle/pallas_call | solution.py:383
  16.8 2.7 %second_apply.1 = (f32[16,2048]{1,0:T(8,128)S(1)}, f32[48,128]{1,0:T(8,128)S(1)}) custom-call(s32[98]{0:T(128)S(1)} %pad_add_fusion.meta_ref, f32[16,2048]{1,0:T(8,128)S(1)} %copy-done.2, f32[32,1024]{1,0:T(8,128)S(1)} %collective-permute-done.left_ref.pleft_ref, f32[32,1024]{1,0:T(8,128)S(1)} %collective-permute-done.1.right_ref.pright_ref, ...), custom_call_target="tpu_custom_call" | custom-call | tf_op jit(solution)/shard_map/second_apply/pallas_call | solution.py:394
  19.5 3.9 %collective-permute-start.4 = (f32[48,128]{1,0:T(8,128)S(1)}, f32[48,128]{1,0:T(8,128)S(1)}, u32[]{:S(2)}, u32[]{:S(2)}) collective-permute-start(f32[48,128]{1,0:T(8,128)S(1)} %get-tuple-element.23.refs_0_), channel_id=1, source_target_pairs={{0,1},{1,0},{2,3},{3,2},{4,5},{5,4},{6,7},{7,6},{8,9},{9,8},{10,11... | collective-permute-start | bytes 73736 | tf_op jit(solution)/shard_map/ppermute | solution.py:411
  23.4 0.8 %collective-permute-done.4.refs_1_ = f32[48,128]{1,0:T(8,128)S(1)} collective-permute-done((f32[48,128]{1,0:T(8,128)S(1)}, f32[48,128]{1,0:T(8,128)S(1)}, u32[]{:S(2)}, u32[]{:S(2)}) %collective-permute-start.4) | collective-permute-done | bytes 24608 | tf_op jit(solution)/shard_map/ppermute | solution.py:411
  24.3 0.2 merge.3.refs_0_
  24.4 2.5 %collective-permute-start.5 = (f32[48,128]{1,0:T(8,128)S(1)}, f32[48,128]{1,0:T(8,128)S(1)}, u32[]{:S(2)}, u32[]{:S(2)}) collective-permute-start(f32[48,128]{1,0:T(8,128)S(1)} %merge.3.refs_0_), channel_id=1, source_target_pairs={{0,2},{1,3},{2,0},{3,1},{4,6},{5,7},{6,4},{7,5},{8,10},{9,11},{10,... | collective-permute-start | bytes 73736 | tf_op jit(solution)/shard_map/ppermute | solution.py:411
  26.9 1.8 %collective-permute-done.5.refs_1_ = f32[48,128]{1,0:T(8,128)S(1)} collective-permute-done((f32[48,128]{1,0:T(8,128)S(1)}, f32[48,128]{1,0:T(8,128)S(1)}, u32[]{:S(2)}, u32[]{:S(2)}) %collective-permute-start.5) | collective-permute-done | bytes 24608 | tf_op jit(solution)/shard_map/ppermute | solution.py:411
  28.7 0.2 merge.4.refs_0_
  28.9 2.1 %collective-permute-start.6 = (f32[48,128]{1,0:T(8,128)S(1)}, f32[48,128]{1,0:T(8,128)S(1)}, u32[]{:S(2)}, u32[]{:S(2)}) collective-permute-start(f32[48,128]{1,0:T(8,128)S(1)} %merge.4.refs_0_), channel_id=1, source_target_pairs={{0,4},{1,5},{2,6},{3,7},{4,0},{5,1},{6,2},{7,3},{8,12},{9,13},{10,... | collective-permute-start | bytes 73736 | tf_op jit(solution)/shard_map/ppermute | solution.py:411
  31.0 1.8 %collective-permute-done.6.refs_1_ = f32[48,128]{1,0:T(8,128)S(1)} collective-permute-done((f32[48,128]{1,0:T(8,128)S(1)}, f32[48,128]{1,0:T(8,128)S(1)}, u32[]{:S(2)}, u32[]{:S(2)}) %collective-permute-start.6) | collective-permute-done | bytes 24608 | tf_op jit(solution)/shard_map/ppermute | solution.py:411
  32.8 0.2 merge.5.refs_0_
  33.0 3.1 %collective-permute-start.7 = (f32[48,128]{1,0:T(8,128)S(1)}, f32[48,128]{1,0:T(8,128)S(1)}, u32[]{:S(2)}, u32[]{:S(2)}) collective-permute-start(f32[48,128]{1,0:T(8,128)S(1)} %merge.5.refs_0_), channel_id=1, source_target_pairs={{0,8},{1,9},{2,10},{3,11},{4,12},{5,13},{6,14},{7,15},{8,0},{9,1},... | collective-permute-start | bytes 73736 | tf_op jit(solution)/shard_map/ppermute | solution.py:411
  36.8 1.2 %collective-permute-done.7.refs_1_ = f32[48,128]{1,0:T(8,128)S(1)} collective-permute-done((f32[48,128]{1,0:T(8,128)S(1)}, f32[48,128]{1,0:T(8,128)S(1)}, u32[]{:S(2)}, u32[]{:S(2)}) %collective-permute-start.7) | collective-permute-done | bytes 24608 | tf_op jit(solution)/shard_map/ppermute | solution.py:411
  37.9 3.7 %finish.1 = (f32[16,2048]{1,0:T(8,128)}, f32[16,2048]{1,0:T(8,128)}, f32[48,48]{1,0:T(8,128)}) custom-call(s32[1]{0:T(128)S(6)} %copy.11.locked_ref, f32[48,128]{1,0:T(8,128)S(1)} %merge.5.refs_0_, f32[48,128]{1,0:T(8,128)S(1)} %collective-permute-done.7.refs_1_, f32[16,2048]{1,0:T(8,128)S(1)} %copy-done, f32[16,2048]{1,0:T(8,128)S(1)} %get-tuple-element.16.ax_ref.refs_3_, ...), custom_call_target="tpu_custom_call" | custom-call | tf_op jit(solution)/shard_map/finish/pallas_call | solution.py:423
  (10 shorter events, 0.0 us)
Async XLA Ops:
  0.7 14.7 %copy-start.2 = (f32[16,2048]{1,0:T(8,128)S(1)}, f32[16,2048]{1,0:T(8,128)}, u32[]{:S(2)}) copy-start(f32[16,2048]{1,0:T(8,128)} %p_ref.3) | copy-start | bytes 393220
  1.7 10.9 %collective-permute-start.1 = (f32[32,1024]{1,0:T(8,128)S(1)}, f32[32,1024]{1,0:T(8,128)S(1)}, u32[]{:S(2)}, u32[]{:S(2)}) collective-permute-start(f32[32,1024]{1,0:T(8,128)S(1)} %pad_maximum_fusion.1), channel_id=1, source_target_pairs={{1,2},{2,1},{3,4},{4,3},{5,6},{6,5},{7,8},{8,7},{9,10},{10,9},{11,... | collective-permute-start | bytes 393224 | tf_op jit(solution)/shard_map/ppermute | solution.py:339
  2.4 10.2 %collective-permute-start = (f32[32,1024]{1,0:T(8,128)S(1)}, f32[32,1024]{1,0:T(8,128)S(1)}, u32[]{:S(2)}, u32[]{:S(2)}) collective-permute-start(f32[32,1024]{1,0:T(8,128)S(1)} %pad_maximum_fusion), channel_id=1, source_target_pairs={{0,1},{1,0},{2,3},{3,2},{4,5},{5,4},{6,7},{7,6},{8,9},{9,8},{10,11... | collective-permute-start | bytes 393224 | tf_op jit(solution)/shard_map/ppermute | solution.py:339
  7.4 0.9 %copy-start = (f32[16,2048]{1,0:T(8,128)S(1)}, f32[16,2048]{1,0:T(8,128)}, u32[]{:S(2)}) copy-start(f32[16,2048]{1,0:T(8,128)} %refs_2_.1) | copy-start | bytes 393220
  8.3 1.9 %copy-start.1 = (f32[48,128,128]{2,1,0:T(8,128)S(1)}, f32[48,128,128]{2,1,0:T(8,128)}, u32[]{:S(2)}) copy-start(f32[48,128,128]{2,1,0:T(8,128)} %tiles_hbm.1) | copy-start | bytes 9437188
  14.6 2.2 %collective-permute-start.2 = (f32[16,1024]{1,0:T(8,128)S(1)}, f32[16,1024]{1,0:T(8,128)S(1)}, u32[]{:S(2)}, u32[]{:S(2)}) collective-permute-start(f32[16,1024]{1,0:T(8,128)S(1)} %get-tuple-element.17), channel_id=1, source_target_pairs={{0,1},{1,0},{2,3},{3,2},{4,5},{5,4},{6,7},{7,6},{8,9},{9,8},{10,11... | collective-permute-start | bytes 196616 | tf_op jit(solution)/shard_map/ppermute | solution.py:339
  14.6 2.1 %collective-permute-start.3 = (f32[16,1024]{1,0:T(8,128)S(1)}, f32[16,1024]{1,0:T(8,128)S(1)}, u32[]{:S(2)}, u32[]{:S(2)}) collective-permute-start(f32[16,1024]{1,0:T(8,128)S(1)} %get-tuple-element.18), channel_id=1, source_target_pairs={{1,2},{2,1},{3,4},{4,3},{5,6},{6,5},{7,8},{8,7},{9,10},{10,9},{11,... | collective-permute-start | bytes 196616 | tf_op jit(solution)/shard_map/ppermute | solution.py:339
  19.5 4.8 %collective-permute-start.4 = (f32[48,128]{1,0:T(8,128)S(1)}, f32[48,128]{1,0:T(8,128)S(1)}, u32[]{:S(2)}, u32[]{:S(2)}) collective-permute-start(f32[48,128]{1,0:T(8,128)S(1)} %get-tuple-element.23.refs_0_), channel_id=1, source_target_pairs={{0,1},{1,0},{2,3},{3,2},{4,5},{5,4},{6,7},{7,6},{8,9},{9,8},{10,11... | collective-permute-start | bytes 73736 | tf_op jit(solution)/shard_map/ppermute | solution.py:411
  24.4 4.3 %collective-permute-start.5 = (f32[48,128]{1,0:T(8,128)S(1)}, f32[48,128]{1,0:T(8,128)S(1)}, u32[]{:S(2)}, u32[]{:S(2)}) collective-permute-start(f32[48,128]{1,0:T(8,128)S(1)} %merge.3.refs_0_), channel_id=1, source_target_pairs={{0,2},{1,3},{2,0},{3,1},{4,6},{5,7},{6,4},{7,5},{8,10},{9,11},{10,... | collective-permute-start | bytes 73736 | tf_op jit(solution)/shard_map/ppermute | solution.py:411
  28.9 3.9 %collective-permute-start.6 = (f32[48,128]{1,0:T(8,128)S(1)}, f32[48,128]{1,0:T(8,128)S(1)}, u32[]{:S(2)}, u32[]{:S(2)}) collective-permute-start(f32[48,128]{1,0:T(8,128)S(1)} %merge.4.refs_0_), channel_id=1, source_target_pairs={{0,4},{1,5},{2,6},{3,7},{4,0},{5,1},{6,2},{7,3},{8,12},{9,13},{10,... | collective-permute-start | bytes 73736 | tf_op jit(solution)/shard_map/ppermute | solution.py:411
  33.0 4.9 %collective-permute-start.7 = (f32[48,128]{1,0:T(8,128)S(1)}, f32[48,128]{1,0:T(8,128)S(1)}, u32[]{:S(2)}, u32[]{:S(2)}) collective-permute-start(f32[48,128]{1,0:T(8,128)S(1)} %merge.5.refs_0_), channel_id=1, source_target_pairs={{0,8},{1,9},{2,10},{3,11},{4,12},{5,13},{6,14},{7,15},{8,0},{9,1},... | collective-permute-start | bytes 73736 | tf_op jit(solution)/shard_map/ppermute | solution.py:411

commit v4 on v3

--- a/solution.py
+++ b/solution.py
@@ -58,11 +58,11 @@
     return y1[:h] + ((y1[h : 2 * h] + y2[:h]) + (y1[2 * h :] + y2[h : 2 * h] + y3))
 
 
-def diagonal_tiles(parts_ref, sums_ref, tiles_ref, height, start, stop):
+def diagonal_tiles(parts_ref, sums_ref, tiles_ref, height, start, stop, offset=0):
     def step(index, carry):
         for u in range(UNROLL):
             t = index * UNROLL + u
-            sums_ref[t] = tile_product(parts_ref, tiles_ref, t, t, height)
+            sums_ref[t] = tile_product(parts_ref, tiles_ref, t, t + offset, height)
         return carry
 
     lax.fori_loop(start // UNROLL, stop // UNROLL, step, 0)
@@ -87,33 +87,17 @@
     lax.fori_loop(0, (slots - row_tiles) // UNROLL, step, 0)
 
 
-def split_kernel(tiles_hbm, x_ref, out_ref, sums_ref, tiles_ref, parts_ref, sems):
-    row_tiles, k_rows, tile = sums_ref.shape
-    slots = tiles_ref.shape[0]
-    chunks = sems.shape[0]
-    size = slots // chunks
-
-    def copy(c):
-        part = pl.ds(c * size, size)
-        return pltpu.make_async_copy(tiles_hbm.at[part], tiles_ref.at[part], sems.at[c])
-
-    for c in range(chunks):
-        copy(c).start()
-    load_middle(parts_ref, 0, 0, k_rows, x_ref, tile)
-    for c in range(chunks):
-        copy(c).wait()
-
-        def step(t, carry):
-            for k, part in enumerate(split3(tiles_ref[t])):
-                out_ref[k, t] = part
-            return carry
-
-        lax.fori_loop(c * size, (c + 1) * size, step, 0, unroll=2)
-        if (c + 1) * size <= row_tiles:
-            diagonal_tiles(parts_ref, sums_ref, out_ref, k_rows, c * size, (c + 1) * size)
-
-
-def first_kernel(tile, meta_ref, x_ref, left_ref, right_ref, tiles_ref, start_ref,
+def split_kernel(tiles_ref, out_ref):
+    def step(t, carry):
+        for u in range(4):
+            for k, part in enumerate(split3(tiles_ref[4 * t + u])):
+                out_ref[k, 4 * t + u] = part
+        return carry
+
+    lax.fori_loop(0, tiles_ref.shape[0] // 4, step, 0)
+
+
+def first_kernel(tile, meta_ref, x_ref, left_ref, right_ref, tiles_ref,
                  image_ref, first_ref, second_ref, parts_ref, sums_ref):
     channels = x_ref.shape[0]
     reach = left_ref.shape[1] // tile
@@ -122,7 +106,7 @@
     load_middle(parts_ref, reach, 0, channels, x_ref, tile)
     load_edges(parts_ref, 0, channels, left_ref.at[0:channels], right_ref.at[0:channels],
                row_tiles, tile, odd)
-    sums_ref[...] = start_ref[...]
+    diagonal_tiles(parts_ref, sums_ref, tiles_ref, channels, 0, row_tiles, reach)
     extra_tiles(parts_ref, sums_ref, tiles_ref, meta_ref, channels, reach)
     for i in range(row_tiles):
         cut = slice(i * tile, (i + 1) * tile)
@@ -353,24 +337,19 @@
     left, right = halo(edge(1 - odd), edge(odd))
     params = pltpu.CompilerParams(vmem_limit_bytes=VMEM_LIMIT)
     cost = pl.CostEstimate(flops=10**8, bytes_accessed=10**7, transcendentals=0)
-    parts, x_sums = pl.pallas_call(
+    parts = pl.pallas_call(
         split_kernel,
-        out_shape=(jax.ShapeDtypeStruct((3, slots, tile, tile), BF16), sds(row_tiles, k, tile)),
-        in_specs=[pl.BlockSpec(memory_space=pltpu.HBM), VMEM],
-        out_specs=(VMEM,) * 2,
-        scratch_shapes=[
-            pltpu.VMEM((slots, tile, tile), F32),
-            pltpu.VMEM((row_tiles, 3 * k, tile), BF16),
-            pltpu.SemaphoreType.DMA((slots // UNROLL,)),
-        ],
+        out_shape=jax.ShapeDtypeStruct((3, slots, tile, tile), BF16),
+        in_specs=[VMEM],
+        out_specs=VMEM,
         compiler_params=params,
         cost_estimate=cost,
         name="split_tiles",
-    )(adjacency_tiles, current_block)
+    )(adjacency_tiles)
     x_image, head, tail = pl.pallas_call(
         functools.partial(first_kernel, tile),
         out_shape=(sds(k, rows_here), sds(k, width), sds(k, width)),
-        in_specs=[SMEM] + [VMEM] * 5,
+        in_specs=[SMEM] + [VMEM] * 4,
         out_specs=(VMEM,) * 3,
         scratch_shapes=[
             pltpu.VMEM((span, 3 * k, tile), BF16),
@@ -378,7 +357,7 @@
         ],
         compiler_params=params,
         name="first_apply",
-    )(meta, current_block, left, right, parts, x_sums)
+    )(meta, current_block, left, right, parts)
     aleft, aright = halo(head, tail)
     sums, basis, quotient, begun = pl.pallas_call(
         functools.partial(middle_kernel, tile),

time: 41.8 us -> 40.6 us (0.971)
  local copies, waits for them, and re-layouts: 3.79 us -> 2.89 us
  other arithmetic: 0.77 us -> 0.1 us
  starting transfers between devices: 17.4 us -> 18 us
    pallas_call x1, Pallas kernels: 1.62 us -> 0.61 us  [body(): pl.pallas_call(split_kernel, out_shape=jax.ShapeDtypeStruct((3, slots, ti...]
    unnamed x6 -> x10, local copies, waits for them, and re-layouts: 2.79 us -> 1.9 us
    pallas_call x1, Pallas kernels: 1.96 us -> 2.63 us  [body(): pl.pallas_call(functools.partial(first_kernel, tile), out_shape=(sds(k, r...]
    concatenate x1, other arithmetic: 0.75 us -> 0.08 us  [body(): jnp.concatenate([tile_rows, tile_cols, tile_count, odd[None].astype(jnp.i...]
    ppermute x4, starting transfers between devices: 11.6 us -> 12.2 us  [body(): lax.ppermute(message, AXES, [(i, i ^ m * stride) for i in range(members)])]
  transfers between devices with their start and end apart: 8 -> 8, of which waited for: 4 -> 4; matrix products, arithmetic and copies ran while one was open for 2% -> 0% of each run, Pallas kernels for 7% -> 5%
where the time goes in v4:
time: 40.6 us; the launch traced here: 40.4 us
  starting transfers between devices  18 us (44%)
  Pallas kernels  11.6 us (29%)
  waiting for transfers between devices  5.72 us (14%)
  local copies, waits for them, and re-layouts  2.89 us (7%)
  between operations  2.13 us (5%)
    ppermute x4, starting transfers between devices, body(): lax.ppermute(message, AXES, [(i, i ^ m * stride) for i in range(members)])  12.2 us
    ppermute x4, starting transfers between devices, halo(): return (lax.ppermute(first, AXES, inner), lax.ppermute(second, AXES, outer))  5.79 us
    ppermute x4, waiting for transfers between devices, body(): lax.ppermute(message, AXES, [(i, i ^ m * stride) for i in range(members)])  5.71 us
    pallas_call x1, Pallas kernels, body(): pl.pallas_call(functools.partial(last_kernel, len(messages), 1.0 / vertex...  3.67 us
    pallas_call x1, Pallas kernels, body(): pl.pallas_call(functools.partial(second_kernel, tile), out_shape=(sds(k,...  2.68 us
    pallas_call x1, Pallas kernels, body(): pl.pallas_call(functools.partial(first_kernel, tile), out_shape=(sds(k, r...  2.63 us
    unnamed x10, local copies, waits for them, and re-layouts  1.9 us
    pallas_call x1, Pallas kernels, body(): pl.pallas_call(functools.partial(middle_kernel, tile), out_shape=(sds(row...  1.44 us
  transfers between devices with their start and end apart: 8, of which 4 were waited for; matrix products, arithmetic and copies ran while one was open for 0% of the time, Pallas kernels for 5%

profile of v4, /device:TPU:0, one launch (start us, length us, event | category | flops | bytes accessed | tf_op | source)
XLA Modules:
  0.0 40.4 jit_solution(1782777162581442588)
XLA Ops:
  0.7 1.0 %constant_dynamic-slice_fusion = (f32[16,1024]{1,0:T(8,128)S(1)}, f32[16,1024]{1,0:T(8,128)S(1)}, f32[16,1024]{1,0:T(8,128)S(1)}, f32[16,1024]{1,0:T(8,128)S(1)}) fusion(f32[16,2048]{1,0:T(8,128)} %p_ref.3, s32[]{:T(128)S(6)} %select_n.17, s32[]{:T(128)S(6)} %select_n.16, f32[16,2048]{1,0:T(8,128)} %refs_2_.1), kind=kLoop, calls=%fused_computation.2 | loop fusion | bytes 524296 | tf_op jit(solution)/shard_map/dynamic_slice | solution.py:331
  1.7 0.7 %collective-permute-start.1 = (f32[32,1024]{1,0:T(8,128)S(1)}, f32[32,1024]{1,0:T(8,128)S(1)}, u32[]{:S(2)}, u32[]{:S(2)}) collective-permute-start(f32[32,1024]{1,0:T(8,128)S(1)} %pad_maximum_fusion.1), channel_id=1, source_target_pairs={{1,2},{2,1},{3,4},{4,3},{5,6},{6,5},{7,8},{8,7},{9,10},{10,9},{11,... | collective-permute-start | bytes 393224 | tf_op jit(solution)/shard_map/ppermute | solution.py:323
  2.4 4.4 %collective-permute-start = (f32[32,1024]{1,0:T(8,128)S(1)}, f32[32,1024]{1,0:T(8,128)S(1)}, u32[]{:S(2)}, u32[]{:S(2)}) collective-permute-start(f32[32,1024]{1,0:T(8,128)S(1)} %pad_maximum_fusion), channel_id=1, source_target_pairs={{0,1},{1,0},{2,3},{3,2},{4,5},{5,4},{6,7},{7,6},{8,9},{9,8},{10,11... | collective-permute-start | bytes 393224 | tf_op jit(solution)/shard_map/ppermute | solution.py:323
  7.4 0.0 copy-start
  7.4 1.9 %copy-done = f32[48,128,128]{2,1,0:T(8,128)S(1)} copy-done((f32[48,128,128]{2,1,0:T(8,128)S(1)}, f32[48,128,128]{2,1,0:T(8,128)}, u32[]{:S(2)}) %copy-start) | copy-done | bytes 3145752
  9.3 0.6 %split_tiles.1.tiles_ref = bf16[3,48,128,128]{3,2,1,0:T(8,128)(2,1)S(1)} custom-call(f32[48,128,128]{2,1,0:T(8,128)S(1)} %copy-done), custom_call_target="tpu_custom_call" | custom-call | flops 100000000 | bytes 10000000 | tf_op jit(solution)/shard_map/split_tiles/pallas_call | solution.py:340
  10.0 0.1 pad_add_fusion.meta_ref
  10.1 2.6 %first_apply.1 = (f32[16,2048]{1,0:T(8,128)S(1)}, f32[16,1024]{1,0:T(8,128)S(1)}, f32[16,1024]{1,0:T(8,128)S(1)}) custom-call(s32[98]{0:T(128)S(1)} %pad_add_fusion.meta_ref, f32[16,2048]{1,0:T(8,128)S(1)} %copy-done.1, f32[32,1024]{1,0:T(8,128)S(1)} %collective-permute-done.left_ref.pleft_ref, f32[32,1024]{1,0:T(8,128)S(1)} %collective-permute-done.1.right_ref.pright_ref, ...), custom_call_target="tpu_custom_call" | custom-call | tf_op jit(solution)/shard_map/first_apply/pallas_call | solution.py:349
  12.7 0.1 collective-permute-start.2
  12.8 0.7 %collective-permute-start.3 = (f32[16,1024]{1,0:T(8,128)S(1)}, f32[16,1024]{1,0:T(8,128)S(1)}, u32[]{:S(2)}, u32[]{:S(2)}) collective-permute-start(f32[16,1024]{1,0:T(8,128)S(1)} %get-tuple-element.14), channel_id=1, source_target_pairs={{1,2},{2,1},{3,4},{4,3},{5,6},{6,5},{7,8},{8,7},{9,10},{10,9},{11,... | collective-permute-start | bytes 196616 | tf_op jit(solution)/shard_map/ppermute | solution.py:323
  13.5 1.4 %middle.1 = (f32[16,32,128]{2,1,0:T(8,128)S(1)}, f32[64,2048]{1,0:T(8,128)S(1)}, f32[16,128]{1,0:T(8,128)S(1)}, f32[48,128]{1,0:T(8,128)S(1)}) custom-call(f32[16,2048]{1,0:T(8,128)S(1)} %copy-done.1, f32[16,2048]{1,0:T(8,128)S(1)} %copy-done.2, f32[16,2048]{1,0:T(8,128)S(1)} %get-tuple-element.12.ax_ref.refs_3_, ...), custom_call_target="tpu_custom_call" | custom-call | flops 100000000 | bytes 10000000 | tf_op jit(solution)/shard_map/middle/pallas_call | solution.py:362
  14.9 2.7 %second_apply.1 = (f32[16,2048]{1,0:T(8,128)S(1)}, f32[48,128]{1,0:T(8,128)S(1)}) custom-call(s32[98]{0:T(128)S(1)} %pad_add_fusion.meta_ref, f32[16,2048]{1,0:T(8,128)S(1)} %copy-done.2, f32[32,1024]{1,0:T(8,128)S(1)} %collective-permute-done.left_ref.pleft_ref, f32[32,1024]{1,0:T(8,128)S(1)} %collective-permute-done.1.right_ref.pright_ref, ...), custom_call_target="tpu_custom_call" | custom-call | tf_op jit(solution)/shard_map/second_apply/pallas_call | solution.py:373
  17.6 4.1 %collective-permute-start.4 = (f32[48,128]{1,0:T(8,128)S(1)}, f32[48,128]{1,0:T(8,128)S(1)}, u32[]{:S(2)}, u32[]{:S(2)}) collective-permute-start(f32[48,128]{1,0:T(8,128)S(1)} %get-tuple-element.19.refs_0_), channel_id=1, source_target_pairs={{0,1},{1,0},{2,3},{3,2},{4,5},{5,4},{6,7},{7,6},{8,9},{9,8},{10,11... | collective-permute-start | bytes 73736 | tf_op jit(solution)/shard_map/ppermute | solution.py:390
  21.7 0.8 %collective-permute-done.4.refs_1_ = f32[48,128]{1,0:T(8,128)S(1)} collective-permute-done((f32[48,128]{1,0:T(8,128)S(1)}, f32[48,128]{1,0:T(8,128)S(1)}, u32[]{:S(2)}, u32[]{:S(2)}) %collective-permute-start.4) | collective-permute-done | bytes 24608 | tf_op jit(solution)/shard_map/ppermute | solution.py:390
  22.6 0.2 merge.3.refs_0_
  22.8 3.1 %collective-permute-start.5 = (f32[48,128]{1,0:T(8,128)S(1)}, f32[48,128]{1,0:T(8,128)S(1)}, u32[]{:S(2)}, u32[]{:S(2)}) collective-permute-start(f32[48,128]{1,0:T(8,128)S(1)} %merge.3.refs_0_), channel_id=1, source_target_pairs={{0,2},{1,3},{2,0},{3,1},{4,6},{5,7},{6,4},{7,5},{8,10},{9,11},{10,... | collective-permute-start | bytes 73736 | tf_op jit(solution)/shard_map/ppermute | solution.py:390
  25.8 1.8 %collective-permute-done.5.refs_1_ = f32[48,128]{1,0:T(8,128)S(1)} collective-permute-done((f32[48,128]{1,0:T(8,128)S(1)}, f32[48,128]{1,0:T(8,128)S(1)}, u32[]{:S(2)}, u32[]{:S(2)}) %collective-permute-start.5) | collective-permute-done | bytes 24608 | tf_op jit(solution)/shard_map/ppermute | solution.py:390
  27.6 0.2 merge.4.refs_0_
  27.8 2.0 %collective-permute-start.6 = (f32[48,128]{1,0:T(8,128)S(1)}, f32[48,128]{1,0:T(8,128)S(1)}, u32[]{:S(2)}, u32[]{:S(2)}) collective-permute-start(f32[48,128]{1,0:T(8,128)S(1)} %merge.4.refs_0_), channel_id=1, source_target_pairs={{0,4},{1,5},{2,6},{3,7},{4,0},{5,1},{6,2},{7,3},{8,12},{9,13},{10,... | collective-permute-start | bytes 73736 | tf_op jit(solution)/shard_map/ppermute | solution.py:390
  29.8 1.9 %collective-permute-done.6.refs_1_ = f32[48,128]{1,0:T(8,128)S(1)} collective-permute-done((f32[48,128]{1,0:T(8,128)S(1)}, f32[48,128]{1,0:T(8,128)S(1)}, u32[]{:S(2)}, u32[]{:S(2)}) %collective-permute-start.6) | collective-permute-done | bytes 24608 | tf_op jit(solution)/shard_map/ppermute | solution.py:390
  31.7 0.2 merge.5.refs_0_
  31.9 3.0 %collective-permute-start.7 = (f32[48,128]{1,0:T(8,128)S(1)}, f32[48,128]{1,0:T(8,128)S(1)}, u32[]{:S(2)}, u32[]{:S(2)}) collective-permute-start(f32[48,128]{1,0:T(8,128)S(1)} %merge.5.refs_0_), channel_id=1, source_target_pairs={{0,8},{1,9},{2,10},{3,11},{4,12},{5,13},{6,14},{7,15},{8,0},{9,1},... | collective-permute-start | bytes 73736 | tf_op jit(solution)/shard_map/ppermute | solution.py:390
  35.6 1.2 %collective-permute-done.7.refs_1_ = f32[48,128]{1,0:T(8,128)S(1)} collective-permute-done((f32[48,128]{1,0:T(8,128)S(1)}, f32[48,128]{1,0:T(8,128)S(1)}, u32[]{:S(2)}, u32[]{:S(2)}) %collective-permute-start.7) | collective-permute-done | bytes 24608 | tf_op jit(solution)/shard_map/ppermute | solution.py:390
  36.7 3.7 %finish.1 = (f32[16,2048]{1,0:T(8,128)}, f32[16,2048]{1,0:T(8,128)}, f32[48,48]{1,0:T(8,128)}) custom-call(s32[1]{0:T(128)S(6)} %copy.11.locked_ref, f32[48,128]{1,0:T(8,128)S(1)} %merge.5.refs_0_, f32[48,128]{1,0:T(8,128)S(1)} %collective-permute-done.7.refs_1_, f32[16,2048]{1,0:T(8,128)S(1)} %copy-done.1, f32[16,2048]{1,0:T(8,128)S(1)} %get-tuple-element.12.ax_ref.refs_3_, ...), custom_call_target="tpu_custom_call" | custom-call | tf_op jit(solution)/shard_map/finish/pallas_call | solution.py:402
  (14 shorter events, 0.0 us)
Async XLA Ops:
  0.6 9.4 %copy-start.1 = (f32[16,2048]{1,0:T(8,128)S(1)}, f32[16,2048]{1,0:T(8,128)}, u32[]{:S(2)}) copy-start(f32[16,2048]{1,0:T(8,128)} %refs_2_.1) | copy-start | bytes 393220
  0.6 9.3 %copy-start.4 = (s32[48]{0:T(128)S(1)}, s32[48]{0:T(128)}, u32[]{:S(2)}) copy-start(s32[48]{0:T(128)} %param.10) | copy-start | bytes 580
  0.7 9.3 %copy-start.3 = (s32[48]{0:T(128)S(1)}, s32[48]{0:T(128)}, u32[]{:S(2)}) copy-start(s32[48]{0:T(128)} %param.11) | copy-start | bytes 580
  1.7 8.3 %collective-permute-start.1 = (f32[32,1024]{1,0:T(8,128)S(1)}, f32[32,1024]{1,0:T(8,128)S(1)}, u32[]{:S(2)}, u32[]{:S(2)}) collective-permute-start(f32[32,1024]{1,0:T(8,128)S(1)} %pad_maximum_fusion.1), channel_id=1, source_target_pairs={{1,2},{2,1},{3,4},{4,3},{5,6},{6,5},{7,8},{8,7},{9,10},{10,9},{11,... | collective-permute-start | bytes 393224 | tf_op jit(solution)/shard_map/ppermute | solution.py:323
  2.4 7.7 %collective-permute-start = (f32[32,1024]{1,0:T(8,128)S(1)}, f32[32,1024]{1,0:T(8,128)S(1)}, u32[]{:S(2)}, u32[]{:S(2)}) collective-permute-start(f32[32,1024]{1,0:T(8,128)S(1)} %pad_maximum_fusion), channel_id=1, source_target_pairs={{0,1},{1,0},{2,3},{3,2},{4,5},{5,4},{6,7},{7,6},{8,9},{9,8},{10,11... | collective-permute-start | bytes 393224 | tf_op jit(solution)/shard_map/ppermute | solution.py:323
  7.4 1.9 %copy-start = (f32[48,128,128]{2,1,0:T(8,128)S(1)}, f32[48,128,128]{2,1,0:T(8,128)}, u32[]{:S(2)}) copy-start(f32[48,128,128]{2,1,0:T(8,128)} %tiles_ref.1) | copy-start | bytes 9437188
  9.3 4.1 %copy-start.2 = (f32[16,2048]{1,0:T(8,128)S(1)}, f32[16,2048]{1,0:T(8,128)}, u32[]{:S(2)}) copy-start(f32[16,2048]{1,0:T(8,128)} %p_ref.3) | copy-start | bytes 393220
  12.7 2.2 %collective-permute-start.2 = (f32[16,1024]{1,0:T(8,128)S(1)}, f32[16,1024]{1,0:T(8,128)S(1)}, u32[]{:S(2)}, u32[]{:S(2)}) collective-permute-start(f32[16,1024]{1,0:T(8,128)S(1)} %get-tuple-element.13), channel_id=1, source_target_pairs={{0,1},{1,0},{2,3},{3,2},{4,5},{5,4},{6,7},{7,6},{8,9},{9,8},{10,11... | collective-permute-start | bytes 196616 | tf_op jit(solution)/shard_map/ppermute | solution.py:323
  12.8 2.1 %collective-permute-start.3 = (f32[16,1024]{1,0:T(8,128)S(1)}, f32[16,1024]{1,0:T(8,128)S(1)}, u32[]{:S(2)}, u32[]{:S(2)}) collective-permute-start(f32[16,1024]{1,0:T(8,128)S(1)} %get-tuple-element.14), channel_id=1, source_target_pairs={{1,2},{2,1},{3,4},{4,3},{5,6},{6,5},{7,8},{8,7},{9,10},{10,9},{11,... | collective-permute-start | bytes 196616 | tf_op jit(solution)/shard_map/ppermute | solution.py:323
  17.6 5.0 %collective-permute-start.4 = (f32[48,128]{1,0:T(8,128)S(1)}, f32[48,128]{1,0:T(8,128)S(1)}, u32[]{:S(2)}, u32[]{:S(2)}) collective-permute-start(f32[48,128]{1,0:T(8,128)S(1)} %get-tuple-element.19.refs_0_), channel_id=1, source_target_pairs={{0,1},{1,0},{2,3},{3,2},{4,5},{5,4},{6,7},{7,6},{8,9},{9,8},{10,11... | collective-permute-start | bytes 73736 | tf_op jit(solution)/shard_map/ppermute | solution.py:390
  22.8 4.9 %collective-permute-start.5 = (f32[48,128]{1,0:T(8,128)S(1)}, f32[48,128]{1,0:T(8,128)S(1)}, u32[]{:S(2)}, u32[]{:S(2)}) collective-permute-start(f32[48,128]{1,0:T(8,128)S(1)} %merge.3.refs_0_), channel_id=1, source_target_pairs={{0,2},{1,3},{2,0},{3,1},{4,6},{5,7},{6,4},{7,5},{8,10},{9,11},{10,... | collective-permute-start | bytes 73736 | tf_op jit(solution)/shard_map/ppermute | solution.py:390
  27.8 3.9 %collective-permute-start.6 = (f32[48,128]{1,0:T(8,128)S(1)}, f32[48,128]{1,0:T(8,128)S(1)}, u32[]{:S(2)}, u32[]{:S(2)}) collective-permute-start(f32[48,128]{1,0:T(8,128)S(1)} %merge.4.refs_0_), channel_id=1, source_target_pairs={{0,4},{1,5},{2,6},{3,7},{4,0},{5,1},{6,2},{7,3},{8,12},{9,13},{10,... | collective-permute-start | bytes 73736 | tf_op jit(solution)/shard_map/ppermute | solution.py:390
  31.9 4.8 %collective-permute-start.7 = (f32[48,128]{1,0:T(8,128)S(1)}, f32[48,128]{1,0:T(8,128)S(1)}, u32[]{:S(2)}, u32[]{:S(2)}) collective-permute-start(f32[48,128]{1,0:T(8,128)S(1)} %merge.5.refs_0_), channel_id=1, source_target_pairs={{0,8},{1,9},{2,10},{3,11},{4,12},{5,13},{6,14},{7,15},{8,0},{9,1},... | collective-permute-start | bytes 73736 | tf_op jit(solution)/shard_map/ppermute | solution.py:390
